TPU v7x, 32 devices: a whole 2x2x4 slice. The times are simulated.
32 devices in a mesh: along: 8 (over z, x), cross: 4 (over y, core).
Axes of the slice: x: 2, y: 2, z: 4, core: 2. Of those that a mesh axis runs over, the one named last changes fastest.
Arguments:
- offsets: float32 [2, 32, 64, 128], P(None, 'along', 'cross'), may hold values from 0 to 1
- velocity: float32 [2, 32, 64, 128], P(None, 'along', 'cross'), may hold values from -6 to 6
- particle_mass: float32 [32, 64, 128], P('along', 'cross'), may hold values from 0.5 to 2
- neighbours: int32 [32, 64, 9], P('along', 'cross'), may hold values from -1 to 8, as said below
- owner_device: int32 [8, 4, 8192, 1], P('along', 'cross'), may hold values from 0 to 31; in each aligned block of 8192 rows (0 to 8191, 8192 to 16383, ..., all dimensions but the last counted through in order) at most 768 rows name the same one
- target_cell: int32 [8, 4, 8192], P('along', 'cross'), may hold values from 0 to 65535
- surface: float32 [3, 1024, 2048], P(None, 'along', 'cross'), may hold values from -6 to 6
- water_depth: float32 [1024, 2048], P('along', 'cross'), may hold values from 0.5 to 2
Outputs:
- grid_state: float32 [3, 1024, 2048], P(None, 'along', 'cross')
- density: float32 [32, 64, 128], P('along', 'cross')
- feedback: float32 [3, 32, 64, 128], P(None, 'along', 'cross')
Inputs may be any that keep to these rules, and one draw needn't show every extreme that they name: `owner_device`: in the rows of one device, at most 768 particles name one owner device (numbered as along index times 4 plus cross index), a bound that some block reaches. `neighbours`: slot 0 holds 4, the tile itself; the other slots hold distinct window positions or -1 for padding.
All inputs are finite; a program needn't handle non-finite values.
Results may differ from a plain program's by a relative error of at most 0.0003.
Values sent between devices are 32-bit elements; how exact they have to be, the bound alone decides.
No kernel may reach another device: no remote copies, remote signals or barrier semaphores. Data moves between devices by JAX's collectives and lax.ppermute only.
A program may use at most 64 MiB of HBM per device.

v0:
```python
import jax
import jax.numpy as jnp
from jax import lax
from jax.sharding import PartitionSpec as P

SUBSTEPS = 4


courant = 0.4
kernel_width = 1.0


def padded_2(cells, sides, width):
    for axis, dim in sides:
        count = lax.axis_size(axis)
        ends = count - 1
        head = lax.slice_in_dim(cells, 0, width, axis=dim)
        tail = lax.slice_in_dim(cells, cells.shape[dim] - width, cells.shape[dim], axis=dim)
        cells = jnp.concatenate(
            [
                lax.ppermute(tail, axis, [(i, (i + 1) % count) for i in range(ends)]),
                cells,
                lax.ppermute(head, axis, [((i + 1) % count, i) for i in range(ends)]),
            ],
            axis=dim,
        )
    return cells


def tile_sums(window_rows, present_row):
    columns = window_rows.shape[2] - 2
    own_row = window_rows[:, 1, 1 : columns + 1, :]
    totals = jnp.zeros((3, columns, window_rows.shape[3]), jnp.float32)
    for window in range(9):
        row_shift = window // 3
        col_shift = window % 3
        nearby = window_rows[:, row_shift, col_shift : col_shift + columns, :]
        delta_x = own_row[0][:, :, None] - nearby[0][:, None, :] - (row_shift - 1.0)
        delta_y = own_row[1][:, :, None] - nearby[1][:, None, :] - (col_shift - 1.0)
        weights = jnp.exp(-(delta_x * delta_x + delta_y * delta_y) / kernel_width)
        weights = weights * present_row[:, window][:, None, None]
        carried = jnp.stack([nearby[4], nearby[4] * nearby[2], nearby[4] * nearby[3]])
        totals = totals + jnp.einsum(
            "tab,ktb->kta", weights, carried, precision=lax.Precision.HIGHEST
        )
    return totals


def particle_pass(padded, neighbours):
    rows = padded.shape[1] - 2
    present = jnp.any(neighbours[..., :, None] == jnp.arange(9, dtype=jnp.int32), axis=-2).astype(
        jnp.float32
    )

    def one_row(row_index):
        window_rows = lax.dynamic_slice_in_dim(padded, row_index, 3, 1)
        present_row = lax.dynamic_index_in_dim(present, row_index, 0, keepdims=False)
        return tile_sums(window_rows, present_row)

    return lax.map(one_row, jnp.arange(rows, dtype=jnp.int32))


def lax_friedrichs(state_pad, depth_pad):
    height = state_pad[0]
    speed_x = state_pad[1]
    speed_y = state_pad[2]
    flux_x = depth_pad * speed_x
    flux_y = depth_pad * speed_y

    def average(quantity):
        return 0.25 * (
            quantity[2:, 1:-1] + quantity[:-2, 1:-1] + quantity[1:-1, 2:] + quantity[1:-1, :-2]
        )

    next_height = average(height) - 0.5 * courant * (
        flux_x[2:, 1:-1] - flux_x[:-2, 1:-1] + flux_y[1:-1, 2:] - flux_y[1:-1, :-2]
    )
    next_speed_x = average(speed_x) - 0.5 * courant * (height[2:, 1:-1] - height[:-2, 1:-1])
    next_speed_y = average(speed_y) - 0.5 * courant * (height[1:-1, 2:] - height[1:-1, :-2])
    return jnp.stack([next_height, next_speed_x, next_speed_y])


def slot_ranks(destination, devices):
    particles = destination.shape[0]
    block = 128
    groups = particles // block
    onehot = (
        destination.reshape(groups, block)[:, :, None] == jnp.arange(devices, dtype=jnp.int32)
    ).astype(jnp.float32)
    lower = (jnp.arange(block)[:, None] > jnp.arange(block)[None, :]).astype(jnp.float32)
    earlier = jnp.einsum("ij,bjd->bid", lower, onehot, precision=lax.Precision.HIGHEST)
    counts = jnp.sum(onehot, axis=1)
    before = jnp.cumsum(counts, axis=0) - counts
    ranks = jnp.sum(onehot * (earlier + before[:, None, :]), axis=2)
    return ranks.reshape(-1).astype(jnp.int32)


def shards(
    offsets, velocity, particle_mass, neighbours, owner_device, target_cell, surface, water_depth
):
    tiles_along = offsets.shape[1]
    tiles_cross = offsets.shape[2]
    tile_size = offsets.shape[3]
    cells_along = surface.shape[1]
    cells_cross = surface.shape[2]
    cell_count = cells_along * cells_cross
    along_count = lax.axis_size("along")
    cross_count = lax.axis_size("cross")
    devices = along_count * cross_count
    stacked = jnp.concatenate([offsets, velocity, particle_mass[None]], axis=0)
    padded = padded_2(stacked, (("along", 1), ("cross", 2)), 1)
    totals = particle_pass(padded, neighbours)
    mass_sum = totals[:, 0]
    density = mass_sum / tile_size
    volume = particle_mass / density
    smooth_x = totals[:, 1] / mass_sum
    smooth_y = totals[:, 2] / mass_sum
    sources = jnp.stack([volume, volume * smooth_x, volume * smooth_y]).reshape(3, -1)
    destination = owner_device.reshape(-1)
    particles = destination.shape[0]
    capacity = 3 * particles // devices
    slot_total = devices * capacity
    slot_index = destination * capacity + slot_ranks(destination, devices)
    payload = jnp.concatenate([target_cell.reshape(1, -1).astype(jnp.float32), sources], axis=0)
    send_index = (
        jnp.arange(4, dtype=jnp.int32)[:, None] * slot_total + slot_index[None, :]
    ).reshape(-1)
    outgoing = jnp.zeros((4 * slot_total,), jnp.float32).at[send_index].set(payload.reshape(-1))
    outgoing = outgoing.reshape(4, devices, capacity)
    incoming = lax.all_to_all(
        outgoing, ("along", "cross"), split_axis=1, concat_axis=1, tiled=True
    ).reshape(4, -1)
    cells_in = incoming[0].astype(jnp.int32)
    cell_index = (jnp.arange(3, dtype=jnp.int32)[:, None] * cell_count + cells_in[None, :]).reshape(
        -1
    )
    grid_source = (
        jnp.zeros((3 * cell_count,), jnp.float32).at[cell_index].add(incoming[1:].reshape(-1))
    )
    grid_source = grid_source.reshape(3, cells_along, cells_cross)
    margin = SUBSTEPS
    wide_state, wide_depth, wide_source = (
        padded_2(surface, (("along", 1), ("cross", 2)), margin),
        padded_2(water_depth[None], (("along", 1), ("cross", 2)), margin),
        padded_2(grid_source, (("along", 1), ("cross", 2)), margin),
    )
    rows_global = (
        lax.axis_index("along") * cells_along
        - margin
        + jnp.arange(cells_along + 2 * margin, dtype=jnp.int32)
    )
    cols_global = (
        lax.axis_index("cross") * cells_cross
        - margin
        + jnp.arange(cells_cross + 2 * margin, dtype=jnp.int32)
    )
    inside_rows = (rows_global >= 0) & (rows_global < cells_along * along_count)
    inside_cols = (cols_global >= 0) & (cols_global < cells_cross * cross_count)
    inside = (inside_rows[:, None] & inside_cols[None, :]).astype(jnp.float32)
    depth_pad = jnp.pad(wide_depth[0], 1)
    for substep in range(SUBSTEPS):
        state_pad = jnp.pad(wide_state, ((0, 0), (1, 1), (1, 1)))
        wide_state = (lax_friedrichs(state_pad, depth_pad) + wide_source) * inside
    water_state = wide_state[:, margin : margin + cells_along, margin : margin + cells_cross]
    looked = water_state.reshape(-1)[cell_index].reshape(3, devices, capacity)
    returned = lax.all_to_all(
        looked, ("along", "cross"), split_axis=1, concat_axis=1, tiled=True
    ).reshape(-1)
    back_index = (
        jnp.arange(3, dtype=jnp.int32)[:, None] * slot_total + slot_index[None, :]
    ).reshape(-1)
    feedback = returned[back_index].reshape(3, tiles_along, tiles_cross, tile_size)
    return (water_state, density, feedback)


def solution(mesh):
    in_specs = (
        P(None, "along", "cross", None),
        P(None, "along", "cross", None),
        P("along", "cross", None),
        P("along", "cross", None),
        P("along", "cross", None, None),
        P("along", "cross", None),
        P(None, "along", "cross"),
        P("along", "cross"),
    )
    out_specs = (
        P(None, "along", "cross"),
        P("along", "cross", None),
        P(None, "along", "cross", None),
    )
    return jax.shard_map(shards, mesh=mesh, in_specs=in_specs, out_specs=out_specs, check_vma=False)
```

profile of v0, /device:TPU:0, one launch (start us, length us, event | category | flops | bytes accessed | tf_op | source)
XLA Modules:
  0.0 1478.4 jit_solution(241931386850964213)
XLA Ops:
  1.4 4.9 collective-permute-start.8
  8.4 4.5 collective-permute-start.4
  15.0 5.0 collective-permute-start
  32.9 4.4 collective-permute-done.1
  37.4 3.9 collective-permute-start.2
  42.8 5.1 collective-permute-start.10
  49.8 2.4 collective-permute-done.11
  52.3 96.8 %while.13 = (s32[]{:T(128)}, f32[4,3,16,128]{3,2,0,1:T(8,128)S(1)}, s32[4]{0:T(128)S(1)}, f32[5,6,18,128]{3,2,1,0:T(8,128)S(1)}, f32[4,16,9]{1,0,2:T(4,128)}, /*...) while((s32[]{:T(128)}, f32[4,3,16,128]{3,2,0,1:T(8,128)S(1)}, ...), condition=%wide.region_5.6_spmd, body=%wide.region_4.5_spmd.sunk | while | flops 104792080 | bytes 2199840 | solution.py:60
  59.7 2.1 convolution_add_fusion.16
  61.8 2.1 convolution_add_fusion.17
  63.9 2.1 convolution_add_fusion.18
  66.0 2.1 convolution_add_fusion.19
  68.1 2.1 convolution_add_fusion.20
  70.2 2.1 convolution_add_fusion.21
  72.3 2.1 convolution_add_fusion.22
  74.5 2.1 fusion.347
  83.8 2.1 convolution_add_fusion.16
  85.9 2.1 convolution_add_fusion.17
  88.0 2.1 convolution_add_fusion.18
  90.1 2.1 convolution_add_fusion.19
  92.2 2.1 convolution_add_fusion.20
  94.3 2.1 convolution_add_fusion.21
  96.4 2.1 convolution_add_fusion.22
  98.6 2.1 fusion.347
  107.9 2.1 convolution_add_fusion.16
  110.0 2.1 convolution_add_fusion.17
  112.1 2.1 convolution_add_fusion.18
  114.2 2.1 convolution_add_fusion.19
  116.3 2.1 convolution_add_fusion.20
  120.5 2.1 convolution_add_fusion.22
  132.0 2.1 convolution_add_fusion.16
  136.2 2.1 convolution_add_fusion.18
  138.3 2.1 convolution_add_fusion.19
  140.4 2.1 convolution_add_fusion.20
  142.5 2.1 convolution_add_fusion.21
  144.6 2.1 convolution_add_fusion.22
  146.7 2.1 fusion.347
  149.9 120.5 %scatter_custom_fusion = f32[98304]{0:T(1024)S(1)} fusion(s32[32768]{0:T(1024)} %bitcast.321, f32[32768]{0:T(1024)S(1)} %bitcast.322, f32[]{:T(128)} %constant.95.clone.1), kind=kCustom, calls=%fused_computation.447 | custom fusion | bytes 393728 | tf_op jit(solution)/shard_map/scatter | solution.py:128
  271.5 7.4 all-to-all-start
  280.8 11.3 all-to-all-done
  293.6 476.7 %scatter_custom_fusion.1 = f32[196608]{0:T(1024)S(1)} fusion(s32[73728]{0:T(1024)S(1)} %bitcast.301, f32[73728]{0:T(1024)S(1)} %reshape.883, f32[]{:T(128)} %constant.95.clone.1), kind=kCustom, calls=%fused_computation.344 | custom fusion | flops 73728 | bytes 786436 | tf_op jit(solution)/shard_map/scatter-add | solution.py:138
  773.6 3.9 collective-permute-done.13
  777.6 12.0 collective-permute-start.14
  791.0 4.6 collective-permute-done.15
  803.9 408.0 %gather_fusion = f32[73728]{0:T(1024)S(1)} fusion(f32[196608]{0:T(1024)S(1)} %bitcast.299, s32[73728]{0:T(1024)S(1)} %broadcast_clamp_fusion), kind=kCustom, calls=%fused_computation | custom fusion | bytes 884736 | tf_op jit(solution)/shard_map/gather | solution.py:165
  1212.9 11.5 all-to-all-start.1
  1224.5 13.2 all-to-all-done.1
  1237.8 240.6 %gather_fusion.1 = f32[24576]{0:T(1024)} fusion(f32[73728]{0:T(1024)S(1)} %reshape.853, s32[24576]{0:T(1024)S(1)} %broadcast_clamp_fusion.1), kind=kCustom, calls=%fused_computation.1 | custom fusion | bytes 294912 | tf_op jit(solution)/shard_map/gather | solution.py:172
  (181 shorter events, 61.3 us)
Async XLA Ops:
  1.4 41.2 %collective-permute-start.8 = (f32[5,1,16,128]{3,2,1,0:T(8,128)S(1)}, f32[5,1,16,128]{3,2,1,0:T(8,128)S(1)}, u32[]{:S(2)}, u32[]{:S(2)}) collective-permute-start(f32[5,1,16,128]{3,2,1,0:T(8,128)S(1)} %get-tuple-element.239), channel_id=1, source_target_pairs={{0,4},{4,8},{8,12},{12,16},{16,20},{20,24},{24,28},{1,5},{5,9},{9,... | collective-permute-start | bytes 122888 | tf_op jit(solution)/shard_map/ppermute | solution.py:21
  6.3 36.4 %collective-permute-start.9 = (f32[5,1,16,128]{3,2,1,0:T(8,128)S(1)}, f32[5,1,16,128]{3,2,1,0:T(8,128)S(1)}, u32[]{:S(2)}, u32[]{:S(2)}) collective-permute-start(f32[5,1,16,128]{3,2,1,0:T(8,128)S(1)} %get-tuple-element.240), channel_id=1, source_target_pairs={{4,0},{8,4},{12,8},{16,12},{20,16},{24,20},{28,24},{5,1},{9,5},{13... | collective-permute-start | bytes 122888 | tf_op jit(solution)/shard_map/ppermute | solution.py:23
  8.4 18.0 %collective-permute-start.4 = (f32[1,4,512]{2,1,0:T(4,128)S(1)}, f32[1,4,512]{2,1,0:T(4,128)S(1)}, u32[]{:S(2)}, u32[]{:S(2)}) collective-permute-start(f32[1,4,512]{2,1,0:T(4,128)S(1)} %get-tuple-element.235), channel_id=1, source_target_pairs={{0,4},{4,8},{8,12},{12,16},{16,20},{20,24},{24,28},{1,5},{5,9},{9,... | collective-permute-start | bytes 24584 | tf_op jit(solution)/shard_map/ppermute | solution.py:21
  12.9 13.4 collective-permute-start.5
  15.0 17.8 %collective-permute-start = (f32[3,4,512]{2,1,0:T(4,128)S(1)}, f32[3,4,512]{2,1,0:T(4,128)S(1)}, u32[]{:S(2)}, u32[]{:S(2)}) collective-permute-start(f32[3,4,512]{2,1,0:T(4,128)S(1)} %get-tuple-element.223), channel_id=1, source_target_pairs={{0,4},{4,8},{8,12},{12,16},{16,20},{20,24},{24,28},{1,5},{5,9},{9,... | collective-permute-start | bytes 73736 | tf_op jit(solution)/shard_map/ppermute | solution.py:21
  24.7 1.5 copy-start.11
  24.7 1.6 copy-start.5
  26.1 11.2 copy-start
  26.4 4.1 collective-permute-start.6
  27.7 4.9 collective-permute-start.7
  30.5 12.2 copy-start.7
  30.5 12.2 copy-start.8
  30.5 12.2 copy-start.9
  30.5 6.8 collective-permute-start.1
  37.4 11.8 collective-permute-start.2
  41.4 7.8 collective-permute-start.3
  42.8 7.0 collective-permute-start.10
  47.9 4.3 collective-permute-start.11
  52.3 97.4 %copy-start.10 = (f32[1,8192]{1,0:T(1,128)S(1)}, f32[1,8192]{1,0:T(1,128)}, u32[]{:S(2)}) copy-start(f32[1,8192]{1,0:T(1,128)} %convert_bitcast_fusion) | copy-start | bytes 98308
  271.5 20.6 %all-to-all-start = ((f32[4,32,768]{2,0,1:T(4,128)}), f32[4,32,768]{2,0,1:T(4,128)S(1)}, u32[]{:S(2)}, u32[]{:S(2)}) async-start(f32[4,32,768]{2,0,1:T(4,128)} %copy.90), calls=%async_computation | async-start | bytes 786432 | tf_op jit(solution)/shard_map/all_to_all | solution.py:130
  292.9 0.7 copy-start.3
  770.5 3.2 collective-permute-start.12
  771.8 5.7 collective-permute-start.13
  773.6 17.4 %copy-start.4 = (s32[73728,1]{0,1:T(1,128)S(1)}, s32[73728,1]{0,1:T(1,128)}, u32[]{:S(2)}) copy-start(s32[73728,1]{0,1:T(1,128)} %copy-done.3) | copy-start | bytes 884740
  773.6 22.1 %copy-start.2 = (f32[1,136,520]{2,1,0:T(8,128)S(1)}, f32[1,136,520]{2,1,0:T(8,128)}, u32[]{:S(2)}) copy-start(f32[1,136,520]{2,1,0:T(8,128)} %get-tuple-element.232) | copy-start | bytes 848644
  777.6 13.4 collective-permute-start.14
  789.7 6.0 collective-permute-start.15
  802.2 1.0 copy-start.6
  803.7 408.2 %copy-start.1 = (f32[3,128,512]{2,1,0:T(8,128)}, f32[3,128,512]{2,1,0:T(8,128)S(1)}, u32[]{:S(2)}) copy-start(f32[3,128,512]{2,1,0:T(8,128)S(1)} %fusion.234) | copy-start | bytes 2359300
  1212.9 24.8 %all-to-all-start.1 = ((f32[3,32,768]{2,0,1:T(4,128)}), f32[3,32,768]{2,0,1:T(4,128)S(1)}, u32[]{:S(2)}, u32[]{:S(2)}) async-start(f32[3,32,768]{2,0,1:T(4,128)} %copy.92), calls=%async_computation.1 | async-start | bytes 786432 | tf_op jit(solution)/shard_map/all_to_all | solution.py:166
where the time goes:
time: 1480 us
  local copies, waits for them, and re-layouts  782 us (53%)
  other arithmetic  495 us (33%)
  matrix products  77 us (5%)
  starting transfers between devices  67.4 us (5%)
  waiting for transfers between devices  40.6 us (3%)
    scatter-add x1, other arithmetic, shards(): jnp.zeros((3 * cell_count,), jnp.float32).at[cell_index]  477 us
    gather x1, local copies, waits for them, and re-layouts, shards(): looked = water_state.reshape(-1)[cell_index].reshape(3, devices, capacity)  408 us
    gather x1, local copies, waits for them, and re-layouts, shards(): returned[back_index].reshape(3, tiles_along, tiles_cross, tile_size)  241 us
    scatter x1, local copies, waits for them, and re-layouts, shards(): jnp.zeros((4 * slot_total,), jnp.float32).at[send_index]  120 us
    dot_general x36, matrix products, tile_sums(): jnp.einsum('tab,ktb->kta', weights, carried, precision=lax.Precision.HIGH...  75.8 us
    ppermute x8, starting transfers between devices, padded_2(): lax.ppermute(tail, axis, [(i, (i + 1) % count) for i in range(ends)])  38 us
  transfers between devices with their start and end apart: 18, of which 7 were waited for; matrix products, arithmetic and copies ran while one was open for 1% of the time, Pallas kernels for 0%

commit v1 on v0

v1 whole, which is shorter than its diff:
```python
import math

import jax
import jax.numpy as jnp
from jax import lax
from jax.experimental import pallas as pl
from jax.experimental.pallas import tpu as pltpu
from jax.sharding import PartitionSpec as P

SUBSTEPS = 4
LANES = 128

courant = 0.4
kernel_width = 1.0
LOG2E = math.log2(math.e) / kernel_width

VMEM_LIMIT = 60 * 1024 * 1024


def split(values):
    high = values.astype(jnp.bfloat16).astype(jnp.float32)
    return high, values - high


def vmem():
    return pl.BlockSpec(memory_space=pltpu.MemorySpace.VMEM)


def smem():
    return pl.BlockSpec(memory_space=pltpu.MemorySpace.SMEM)


def columns_of(row):
    return jnp.broadcast_to(row, (LANES, row.shape[1])).T


def sph_kernel(present_ref, pad_ref, density_ref, source_ref, uv_ref, carry_ref, col_ref, acc_ref, sums_ref):
    _, rows2, cols2, size = pad_ref.shape
    rows, cols = rows2 - 2, cols2 - 2
    tiles = rows * cols
    x, y, vx, vy, m = [pad_ref[k] for k in range(5)]
    for d in range(3):
        uv_ref[d] = (2.0 * LOG2E) * (x + (d - 1.0))
        uv_ref[3 + d] = (2.0 * LOG2E) * (y + (d - 1.0))
    gx = [jnp.exp2(-LOG2E * (x + (d - 1.0)) * (x + (d - 1.0))) for d in range(3)]
    gy = [jnp.exp2(-LOG2E * (y + (d - 1.0)) * (y + (d - 1.0))) for d in range(3)]
    for di in range(3):
        for dj in range(3):
            g = gx[di] * gy[dj] * m
            carry_ref[3 * (3 * di + dj)] = g
            carry_ref[3 * (3 * di + dj) + 1] = g * vx
            carry_ref[3 * (3 * di + dj) + 2] = g * vy

    def prepare(t, slot):
        i, j = t // cols, t % cols
        for k in range(2):
            col_ref[slot, k] = columns_of(pad_ref[k, i + 1, pl.ds(j + 1, 1), :])

    def finish(t, slot):
        for k in range(3):
            sums_ref[k, pl.ds(t, 1), :] = jnp.sum(acc_ref[slot, k].T, axis=0, keepdims=True)

    def compute(t, slot):
        i, j = t // cols, t % cols
        half = size // 2
        for h in range(2):
            xa = col_ref[slot, 0, h * half : (h + 1) * half, :]
            ya = col_ref[slot, 1, h * half : (h + 1) * half, :]
            acc = [jnp.zeros((half, size), jnp.float32) for _ in range(3)]
            for w in range(9):
                di, dj = w // 3, w % 3
                there = present_ref[t * 9 + w]
                u = uv_ref[di, i + di, pl.ds(j + dj, 1), :]
                v = uv_ref[3 + dj, i + di, pl.ds(j + dj, 1), :]
                weight = jnp.exp2(xa * u + ya * v)
                for k in range(3):
                    acc[k] = acc[k] + weight * (carry_ref[3 * w + k, i + di, pl.ds(j + dj, 1), :] * there)
            for k in range(3):
                acc_ref[slot, k, h * half : (h + 1) * half, :] = acc[k]

    prepare(0, 0)

    def step(t, _):
        slot = t % 2

        prepare(jnp.minimum(t + 1, tiles - 1), 1 - slot)
        finish(jnp.maximum(t - 1, 0), 1 - slot)
        compute(t, slot)
        return 0

    lax.fori_loop(0, tiles, step, 0)
    finish(tiles - 1, (tiles - 1) % 2)

    for i in range(rows):
        own = pad_ref[:, i + 1, 1 : cols + 1, :]
        outer = jnp.exp2(-LOG2E * (own[0] * own[0] + own[1] * own[1]))
        s0 = outer * sums_ref[0, i * cols : (i + 1) * cols, :]
        s1 = outer * sums_ref[1, i * cols : (i + 1) * cols, :]
        s2 = outer * sums_ref[2, i * cols : (i + 1) * cols, :]
        density = s0 / size
        volume = own[4] / density
        density_ref[i] = density
        source_ref[0, i * cols : (i + 1) * cols, :] = volume
        source_ref[1, i * cols : (i + 1) * cols, :] = volume * (s1 / s0)
        source_ref[2, i * cols : (i + 1) * cols, :] = volume * (s2 / s0)


def sph(padded, present):
    _, rows2, cols2, size = padded.shape
    rows, cols = rows2 - 2, cols2 - 2
    return pl.pallas_call(
        sph_kernel,
        out_shape=(
            jax.ShapeDtypeStruct((rows, cols, size), jnp.float32),
            jax.ShapeDtypeStruct((3, rows * cols, size), jnp.float32),
        ),
        in_specs=[smem(), vmem()],
        out_specs=(vmem(), vmem()),
        scratch_shapes=[
            pltpu.VMEM((6, rows2, cols2, size), jnp.float32),
            pltpu.VMEM((27, rows2, cols2, size), jnp.float32),
            pltpu.VMEM((2, 2, size, size), jnp.float32),
            pltpu.VMEM((2, 3, size, size), jnp.float32),
            pltpu.VMEM((3, rows * cols, size), jnp.float32),
        ],
        compiler_params=pltpu.CompilerParams(vmem_limit_bytes=VMEM_LIMIT),
        name="sph",
    )(present, padded)


def pack_kernel(source_ref, cell_ref, dest_ref, rank_ref, out_ref, left_ref, right_ref, acc_ref, *, group):
    tiles, size = cell_ref.shape
    devices = out_ref.shape[0]
    capacity = right_ref.shape[1]
    acc_ref[...] = jnp.zeros_like(acc_ref)

    def step(b, _):
        for s in range(group):
            t = b * group + s
            at = slice(s * size, (s + 1) * size)
            cell = cell_ref[pl.ds(t, 1), :].astype(jnp.float32)
            upper = jnp.floor(cell * (1.0 / 256.0))
            values = [upper, cell - 256.0 * upper]
            for k in range(3):
                values.extend(split(source_ref[k, pl.ds(t, 1), :]))
            mine = dest_ref[pl.ds(t, 1), :] == lax.broadcasted_iota(jnp.int32, (devices, size), 0)
            for c, value in enumerate(values):
                left_ref[c * devices : (c + 1) * devices, at] = jnp.where(mine, value, 0.0).astype(jnp.bfloat16)
            rank = columns_of(rank_ref[pl.ds(t, 1), :])
            for c in range(capacity // LANES):
                lane = lax.broadcasted_iota(jnp.int32, (size, LANES), 1) + c * LANES
                right_ref[at, c * LANES : (c + 1) * LANES] = jnp.where(rank == lane, 1.0, 0.0).astype(jnp.bfloat16)
        acc_ref[...] += jnp.dot(left_ref[...], right_ref[...], preferred_element_type=jnp.float32)
        return 0

    lax.fori_loop(0, tiles // group, step, 0)

    def part(c):
        return acc_ref[c * devices : (c + 1) * devices, :]

    out_ref[:, 0:capacity] = 256.0 * part(0) + part(1)
    for k in range(3):
        out_ref[:, (k + 1) * capacity : (k + 2) * capacity] = part(2 + 2 * k) + part(3 + 2 * k)


def pack(source, cell, dest, rank, devices, capacity):
    tiles, size = cell.shape
    group = math.gcd(8, tiles)
    return pl.pallas_call(
        lambda *refs: pack_kernel(*refs, group=group),
        out_shape=jax.ShapeDtypeStruct((devices, 4 * capacity), jnp.float32),
        in_specs=[vmem()] * 4,
        out_specs=vmem(),
        scratch_shapes=[
            pltpu.VMEM((8 * devices, group * size), jnp.bfloat16),
            pltpu.VMEM((group * size, capacity), jnp.bfloat16),
            pltpu.VMEM((8 * devices, capacity), jnp.float32),
        ],
        compiler_params=pltpu.CompilerParams(vmem_limit_bytes=VMEM_LIMIT),
        name="pack",
    )(source, cell, dest, rank)


def row_and_col(cell, cells_cross):
    row = jnp.floor((cell + 0.5) * (1.0 / cells_cross))
    return row.astype(jnp.int32), (cell - cells_cross * row).astype(jnp.int32)


def by_load(count, blocks, block, body):
    for n in range(1, blocks + 1):
        low = (n - 1) * block
        fits = (count > low) if n == blocks else (count > low) & (count <= low + block)
        pl.when(fits)(lambda n=n: body(n))


def deposit_kernel(count_ref, in_ref, out_ref, left_ref, right_ref, *, capacity, block):
    _, cells_along, cells_cross = out_ref.shape
    out_ref[...] = jnp.zeros_like(out_ref)

    def sender(s, _):
        def body(n):
            for b in range(n):
                at = slice(b * block, (b + 1) * block)
                row, col = row_and_col(in_ref[pl.ds(s, 1), at], cells_cross)
                mine = row == lax.broadcasted_iota(jnp.int32, (cells_along, block), 0)
                for k in range(3):
                    first = (k + 1) * capacity + b * block
                    for h, value in enumerate(split(in_ref[pl.ds(s, 1), first : first + block])):
                        q = 2 * k + h
                        left_ref[q * cells_along : (q + 1) * cells_along, at] = jnp.where(mine, value, 0.0).astype(
                            jnp.bfloat16
                        )
                for g in range(block // LANES):
                    column = columns_of(col[:, g * LANES : (g + 1) * LANES])
                    for c in range(cells_cross // LANES):
                        lane = lax.broadcasted_iota(jnp.int32, (LANES, LANES), 1) + c * LANES
                        right_ref[b * block + g * LANES : b * block + (g + 1) * LANES, c * LANES : (c + 1) * LANES] = (
                            jnp.where(column == lane, 1.0, 0.0).astype(jnp.bfloat16)
                        )
            for k in range(3):
                both = jnp.dot(
                    left_ref[2 * k * cells_along : (2 * k + 2) * cells_along, 0 : n * block],
                    right_ref[0 : n * block, :],
                    preferred_element_type=jnp.float32,
                )
                out_ref[k] += both[:cells_along] + both[cells_along:]

        by_load(count_ref[s], capacity // block, block, body)
        return 0

    lax.fori_loop(0, in_ref.shape[0], sender, 0)


def deposit(incoming, counts, capacity, cells_along, cells_cross):
    block = math.gcd(256, capacity)
    return pl.pallas_call(
        lambda *refs: deposit_kernel(*refs, capacity=capacity, block=block),
        out_shape=jax.ShapeDtypeStruct((3, cells_along, cells_cross), jnp.float32),
        in_specs=[smem(), vmem()],
        out_specs=vmem(),
        scratch_shapes=[
            pltpu.VMEM((6 * cells_along, capacity), jnp.bfloat16),
            pltpu.VMEM((capacity, cells_cross), jnp.bfloat16),
        ],
        compiler_params=pltpu.CompilerParams(vmem_limit_bytes=VMEM_LIMIT),
        name="deposit",
    )(counts, incoming)


def lookup_kernel(count_ref, in_ref, state_ref, out_ref, left_ref, *, capacity, block):
    _, cells_along, cells_cross = state_ref.shape
    for k in range(3):
        for h, value in enumerate(split(state_ref[k])):
            q = 2 * k + h
            left_ref[q * cells_along : (q + 1) * cells_along, :] = value.astype(jnp.bfloat16)
    out_ref[...] = jnp.zeros_like(out_ref)

    def sender(s, _):
        def body(n):
            for b in range(n):
                row, col = row_and_col(in_ref[pl.ds(s, 1), b * block : (b + 1) * block], cells_cross)
                mine = row == lax.broadcasted_iota(jnp.int32, (cells_along, block), 0)
                right = jnp.where(
                    col == lax.broadcasted_iota(jnp.int32, (cells_cross, block), 0), 1.0, 0.0
                ).astype(jnp.bfloat16)
                for k in range(3):
                    both = jnp.dot(
                        left_ref[2 * k * cells_along : (2 * k + 2) * cells_along, :],
                        right,
                        preferred_element_type=jnp.float32,
                    )
                    chosen = jnp.where(mine, both[:cells_along] + both[cells_along:], 0.0)
                    first = k * capacity + b * block
                    out_ref[pl.ds(s, 1), first : first + block] = jnp.sum(chosen, axis=0, keepdims=True)

        by_load(count_ref[s], capacity // block, block, body)
        return 0

    lax.fori_loop(0, in_ref.shape[0], sender, 0)


def lookup(incoming, counts, state, capacity):
    devices = incoming.shape[0]
    _, cells_along, cells_cross = state.shape
    block = math.gcd(256, capacity)
    return pl.pallas_call(
        lambda *refs: lookup_kernel(*refs, capacity=capacity, block=block),
        out_shape=jax.ShapeDtypeStruct((devices, 3 * capacity), jnp.float32),
        in_specs=[smem(), vmem(), vmem()],
        out_specs=vmem(),
        scratch_shapes=[pltpu.VMEM((6 * cells_along, cells_cross), jnp.bfloat16)],
        compiler_params=pltpu.CompilerParams(vmem_limit_bytes=VMEM_LIMIT),
        name="lookup",
    )(counts, incoming, state)


def unpack_kernel(in_ref, dest_ref, rank_ref, out_ref, left_ref, *, capacity, group):
    tiles, size = dest_ref.shape
    devices = in_ref.shape[0]
    for k in range(3):
        for h, value in enumerate(split(in_ref[:, k * capacity : (k + 1) * capacity])):
            q = 2 * k + h
            left_ref[q * devices : (q + 1) * devices, :] = value.astype(jnp.bfloat16)

    def step(b, _):
        for s in range(group):
            t = b * group + s
            right = jnp.where(
                rank_ref[pl.ds(t, 1), :] == lax.broadcasted_iota(jnp.int32, (capacity, size), 0), 1.0, 0.0
            ).astype(jnp.bfloat16)
            mine = dest_ref[pl.ds(t, 1), :] == lax.broadcasted_iota(jnp.int32, (devices, size), 0)
            every = jnp.dot(left_ref[...], right, preferred_element_type=jnp.float32)
            for k in range(3):
                both = every[2 * k * devices : (2 * k + 1) * devices] + every[(2 * k + 1) * devices : (2 * k + 2) * devices]
                out_ref[k, pl.ds(t, 1), :] = jnp.sum(jnp.where(mine, both, 0.0), axis=0, keepdims=True)
        return 0

    lax.fori_loop(0, tiles // group, step, 0)


def unpack(returned, dest, rank, capacity):
    tiles, size = dest.shape
    devices = returned.shape[0]
    group = math.gcd(4, tiles)
    return pl.pallas_call(
        lambda *refs: unpack_kernel(*refs, capacity=capacity, group=group),
        out_shape=jax.ShapeDtypeStruct((3, tiles, size), jnp.float32),
        in_specs=[vmem()] * 3,
        out_specs=vmem(),
        scratch_shapes=[pltpu.VMEM((6 * devices, capacity), jnp.bfloat16)],
        compiler_params=pltpu.CompilerParams(vmem_limit_bytes=VMEM_LIMIT),
        name="unpack",
    )(returned, dest, rank)


def swap(axis, to_next, to_previous):
    count = lax.axis_size(axis)
    before = lax.ppermute(to_next, axis, [(i, i + 1) for i in range(count - 1)])
    after = lax.ppermute(to_previous, axis, [(i + 1, i) for i in range(count - 1)])
    return before, after


def padded_together(fields):
    arrays = [array for array, _, _ in fields]
    for step, axis in enumerate(("along", "cross")):
        heads, tails = [], []
        for array, (_, dims, width) in zip(arrays, fields):
            dim = dims[step]
            heads.append(lax.slice_in_dim(array, 0, width, axis=dim))
            tails.append(lax.slice_in_dim(array, array.shape[dim] - width, array.shape[dim], axis=dim))
        flat = lambda parts: jnp.concatenate([part.reshape(-1) for part in parts])
        before, after = swap(axis, flat(tails), flat(heads))
        start, grown = 0, []
        for array, head, (_, dims, _) in zip(arrays, heads, fields):
            rims = [rim[start : start + head.size].reshape(head.shape) for rim in (before, after)]
            start += head.size
            grown.append(jnp.concatenate([rims[0], array, rims[1]], axis=dims[step]))
        arrays = grown
    return arrays


def lax_friedrichs(state_pad, depth_pad):
    height = state_pad[0]
    speed_x = state_pad[1]
    speed_y = state_pad[2]
    flux_x = depth_pad * speed_x
    flux_y = depth_pad * speed_y

    def average(quantity):
        return 0.25 * (quantity[2:, 1:-1] + quantity[:-2, 1:-1] + quantity[1:-1, 2:] + quantity[1:-1, :-2])

    next_height = average(height) - 0.5 * courant * (
        flux_x[2:, 1:-1] - flux_x[:-2, 1:-1] + flux_y[1:-1, 2:] - flux_y[1:-1, :-2]
    )
    next_speed_x = average(speed_x) - 0.5 * courant * (height[2:, 1:-1] - height[:-2, 1:-1])
    next_speed_y = average(speed_y) - 0.5 * courant * (height[1:-1, 2:] - height[1:-1, :-2])
    return jnp.stack([next_height, next_speed_x, next_speed_y])


def slot_ranks(destination, devices):
    groups, block = destination.shape
    onehot = (destination[:, :, None] == jnp.arange(devices, dtype=jnp.int32)).astype(jnp.bfloat16)
    lower = (jnp.arange(block)[:, None] > jnp.arange(block)[None, :]).astype(jnp.bfloat16)
    earlier = jnp.einsum("ij,bjd->bid", lower, onehot, preferred_element_type=jnp.float32)
    counts = jnp.sum(onehot.astype(jnp.float32), axis=1)
    before = jnp.cumsum(counts, axis=0) - counts
    return jnp.sum(onehot.astype(jnp.float32) * (earlier + before[:, None, :]), axis=2).astype(jnp.int32)


def shards(offsets, velocity, particle_mass, neighbours, owner_device, target_cell, surface, water_depth):
    _, tiles_along, tiles_cross, tile_size = offsets.shape
    _, cells_along, cells_cross = surface.shape
    along_count = lax.axis_size("along")
    cross_count = lax.axis_size("cross")
    devices = along_count * cross_count
    tiles = tiles_along * tiles_cross
    particles = tiles * tile_size
    capacity = -(-3 * particles // devices // LANES) * LANES
    margin = SUBSTEPS

    stacked = jnp.concatenate([offsets, velocity, particle_mass[None]], axis=0)
    water = jnp.concatenate([surface, water_depth[None]], axis=0)
    padded, wide_water = padded_together([(stacked, (1, 2), 1), (water, (1, 2), margin)])

    destination = owner_device.reshape(tiles, tile_size)
    cell = target_cell.reshape(tiles, tile_size)
    rank = slot_ranks(destination, devices)
    present = jnp.any(neighbours[..., :, None] == jnp.arange(9, dtype=jnp.int32), axis=-2).astype(jnp.float32)

    density, sources = sph(padded, present.reshape(-1))
    outgoing = pack(sources, cell, destination, rank, devices, capacity)
    incoming = lax.all_to_all(outgoing, ("along", "cross"), split_axis=0, concat_axis=0, tiled=True)
    counts = jnp.sum((incoming[:, capacity : 2 * capacity] != 0.0).astype(jnp.int32), axis=1)
    grid_source = deposit(incoming, counts, capacity, cells_along, cells_cross)
    (wide_source,) = padded_together([(grid_source, (1, 2), margin)])

    rows_global = (
        lax.axis_index("along") * cells_along - margin + jnp.arange(cells_along + 2 * margin, dtype=jnp.int32)
    )
    cols_global = (
        lax.axis_index("cross") * cells_cross - margin + jnp.arange(cells_cross + 2 * margin, dtype=jnp.int32)
    )
    inside_rows = (rows_global >= 0) & (rows_global < cells_along * along_count)
    inside_cols = (cols_global >= 0) & (cols_global < cells_cross * cross_count)
    inside = (inside_rows[:, None] & inside_cols[None, :]).astype(jnp.float32)
    wide_state = wide_water[:3]
    depth_pad = jnp.pad(wide_water[3], 1)
    for _ in range(SUBSTEPS):
        state_pad = jnp.pad(wide_state, ((0, 0), (1, 1), (1, 1)))
        wide_state = (lax_friedrichs(state_pad, depth_pad) + wide_source) * inside
    water_state = wide_state[:, margin : margin + cells_along, margin : margin + cells_cross]

    looked = lookup(incoming, counts, water_state, capacity)
    returned = lax.all_to_all(looked, ("along", "cross"), split_axis=0, concat_axis=0, tiled=True)
    feedback = unpack(returned, destination, rank, capacity)
    return water_state, density, feedback.reshape(3, tiles_along, tiles_cross, tile_size)


def solution(mesh):
    in_specs = (
        P(None, "along", "cross", None),
        P(None, "along", "cross", None),
        P("along", "cross", None),
        P("along", "cross", None),
        P("along", "cross", None, None),
        P("along", "cross", None),
        P(None, "along", "cross"),
        P("along", "cross"),
    )
    out_specs = (
        P(None, "along", "cross"),
        P("along", "cross", None),
        P(None, "along", "cross", None),
    )
    return jax.shard_map(shards, mesh=mesh, in_specs=in_specs, out_specs=out_specs, check_vma=False)
```

time: 1480 us -> 188 us (0.13)
  local copies, waits for them, and re-layouts: 782 us -> 11.2 us
  other arithmetic: 495 us -> 16 us
  matrix products: 77 us -> 0.46 us
  Pallas kernels: 0 us -> 74.1 us
  starting transfers between devices: 67.4 us -> 35.7 us
  blocking collectives: 0 us -> 30.4 us
  waiting for transfers between devices: 40.6 us -> 18.8 us
    gather x2 -> x0, local copies, waits for them, and re-layouts: 649 us -> none  [the longest x1 408 us: shards(): looked = water_state.reshape(-1)[cell_index].reshape(3, devices, capacity)]
    scatter-add x1 -> x0, other arithmetic: 477 us -> none  [shards(): jnp.zeros((3 * cell_count,), jnp.float32).at[cell_index]]
    scatter x1 -> x0, local copies, waits for them, and re-layouts: 120 us -> none  [shards(): jnp.zeros((4 * slot_total,), jnp.float32).at[send_index]]
    dot_general x37 -> x1, matrix products: 77 us -> 0.46 us  [slot_ranks(): jnp.einsum('ij,bjd->bid', lower, onehot, preferred_element_type=jnp.float32)]
    pallas_call x0 -> x5, Pallas kernels: none -> 74.1 us  [the longest x1 21.2 us: sph(): pl.pallas_call(sph_kernel, out_shape=(jax.ShapeDtypeStruct((rows, cols, s...]
    all_to_all x0 -> x1, blocking collectives: none -> 30.4 us  [shards(): lax.all_to_all(looked, ('along', 'cross'), split_axis=0, concat_axis=0, t...]
    ppermute x16 -> x8, starting transfers between devices: 48.5 us -> 28.5 us  [the longest x4 23.2 us: swap(): before = lax.ppermute(to_next, axis, [(i, i + 1) for i in range(count - 1)])]
    all_to_all x2 -> x1, waiting for transfers between devices: 24.5 us -> 9.34 us  [shards(): lax.all_to_all(outgoing, ('along', 'cross'), split_axis=0, concat_axis=0,...]
  transfers between devices with their start and end apart: 18 -> 9, of which waited for: 7 -> 5; matrix products, arithmetic and copies ran while one was open for 1% -> 5% of each run, Pallas kernels for 0% -> 0%
where the time goes in v1:
time: 188 us
  Pallas kernels  74.1 us (39%)
  starting transfers between devices  35.7 us (19%)
  blocking collectives  30.4 us (16%)
  waiting for transfers between devices  18.8 us (10%)
  other arithmetic  16 us (9%)
  local copies, waits for them, and re-layouts  11.2 us (6%)
    all_to_all x1, blocking collectives, shards(): lax.all_to_all(looked, ('along', 'cross'), split_axis=0, concat_axis=0, t...  30.4 us
    ppermute x4, starting transfers between devices, swap(): before = lax.ppermute(to_next, axis, [(i, i + 1) for i in range(count - 1)])  23.2 us
    pallas_call x1, Pallas kernels, sph(): pl.pallas_call(sph_kernel, out_shape=(jax.ShapeDtypeStruct((rows, cols, s...  21.2 us
    pallas_call x1, Pallas kernels, deposit(): pl.pallas_call(lambda *refs: deposit_kernel(*refs, capacity=capacity, blo...  18.3 us
    pallas_call x1, Pallas kernels, lookup(): pl.pallas_call(lambda *refs: lookup_kernel(*refs, capacity=capacity, bloc...  15.3 us
    pallas_call x1, Pallas kernels, pack(): pl.pallas_call(lambda *refs: pack_kernel(*refs, group=group), out_shape=j...  10 us
    ppermute x4, waiting for transfers between devices, swap(): lax.ppermute(to_previous, axis, [(i + 1, i) for i in range(count - 1)])  9.45 us
    all_to_all x1, waiting for transfers between devices, shards(): lax.all_to_all(outgoing, ('along', 'cross'), split_axis=0, concat_axis=0,...  9.34 us
  transfers between devices with their start and end apart: 9, of which 5 were waited for; matrix products, arithmetic and copies ran while one was open for 5% of the time, Pallas kernels for 0%

profile of v1, /device:TPU:0, one launch (start us, length us, event | category | flops | bytes accessed | tf_op | source)
XLA Modules:
  0.0 187.8 jit_solution(6702171132170836814)
XLA Ops:
  0.7 0.9 maximum_bitcast_fusion.1
  1.7 5.0 %collective-permute-start = (f32[18432]{0:T(1024)S(1)}, f32[18432]{0:T(1024)S(1)}, u32[]{:S(2)}, u32[]{:S(2)}) collective-permute-start(f32[18432]{0:T(1024)S(1)} %pad_maximum_fusion.12), channel_id=1, source_target_pairs={{0,4},{4,8},{8,12},{12,16},{16,20},{20,24},{24,28},{1,5},{5,9},{9,... | collective-permute-start | bytes 221192 | tf_op jit(solution)/shard_map/ppermute | solution.py:338
  6.8 1.3 collective-permute-start.1
  8.6 0.5 fusion.2
  9.1 3.9 %collective-permute-done.1 = f32[18432]{0:T(1024)S(1)} collective-permute-done((f32[18432]{0:T(1024)S(1)}, f32[18432]{0:T(1024)S(1)}, u32[]{:S(2)}, u32[]{:S(2)}) %collective-permute-start.1) | collective-permute-done | bytes 73760 | tf_op jit(solution)/shard_map/ppermute | solution.py:339
  13.5 1.3 collective-permute-start.2
  15.0 1.3 collective-permute-start.3
  16.5 0.7 reshape.195.present_ref
  17.2 0.6 convert_element_type.39.refs_3_.refs_2_
  17.8 2.1 %collective-permute-done.3 = f32[6016]{0:T(1024)S(1)} collective-permute-done((f32[6016]{0:T(1024)S(1)}, f32[6016]{0:T(1024)S(1)}, u32[]{:S(2)}, u32[]{:S(2)}) %collective-permute-start.3) | collective-permute-done | bytes 24096 | tf_op jit(solution)/shard_map/ppermute | solution.py:339
  19.9 0.8 pad_maximum_fusion.4.pad_ref
  20.7 21.2 %sph.1 = (f32[4,16,128]{2,1,0:T(8,128)}, f32[3,64,128]{2,1,0:T(8,128)}) custom-call(f32[576]{0:T(1024)} %reshape.195.present_ref, f32[5,6,18,128]{3,2,1,0:T(8,128)} %pad_maximum_fusion.4.pad_ref), custom_call_target="tpu_custom_call" | custom-call | tf_op jit(solution)/shard_map/sph/pallas_call | solution.py:111
  41.9 10.0 %pack.1 = f32[32,3072]{1,0:T(8,128)} custom-call(f32[3,64,128]{2,1,0:T(8,128)} %get-tuple-element.5.refs_0_, s32[64,128]{1,0:T(8,128)} %bitcast.130, s32[64,128]{1,0:T(8,128)} %bitcast.118, s32[64,128]{1,0:T(8,128)} %convert_element_type.39.refs_3_.refs_2_), custom_call_target="tpu_custom_call" | custom-call | tf_op jit(solution)/shard_map/pack/pallas_call | solution.py:169
  51.9 2.1 %copy.17 = f32[32,1,3072]{2,1,0:T(1,128)} copy(f32[32,1,3072]{2,0,1:T(8,128)} %bitcast.111) | data formatting | bytes 786432 | tf_op jit(solution)/shard_map/all_to_all | solution.py:412
  54.1 7.1 %all-to-all-start = ((f32[32,1,3072]{2,1,0:T(1,128)}), f32[32,1,3072]{2,1,0:T(1,128)}, u32[]{:S(2)}, u32[]{:S(2)}) async-start(f32[32,1,3072]{2,1,0:T(1,128)} %copy.17), calls=%async_computation | async-start | bytes 786432 | tf_op jit(solution)/shard_map/all_to_all | solution.py:412
  61.3 0.8 slice.537
  62.7 0.6 pad_maximum_fusion
  63.6 1.1 pad_multiply_fusion.7
  65.1 9.3 %all-to-all-done = f32[32,1,3072]{2,1,0:T(1,128)} async-done(((f32[32,1,3072]{2,1,0:T(1,128)}), f32[32,1,3072]{2,1,0:T(1,128)}, u32[]{:S(2)}, u32[]{:S(2)}) %all-to-all-start) | async-done | bytes 393248 | tf_op jit(solution)/shard_map/all_to_all | solution.py:412
  74.4 1.1 copy.27
  75.6 0.6 convert_reduce_fusion.1.refs_0_
  76.3 18.3 %deposit.1 = f32[3,128,512]{2,1,0:T(8,128)} custom-call(s32[32]{0:T(128)} %convert_reduce_fusion.1.refs_0_, f32[32,3072]{1,0:T(8,128)} %bitcast.109), custom_call_target="tpu_custom_call" | custom-call | tf_op jit(solution)/shard_map/deposit/pallas_call | solution.py:236
  94.6 0.8 slice_bitcast_fusion.1
  95.4 15.6 %collective-permute-start.4 = (f32[6144]{0:T(1024)S(1)}, f32[6144]{0:T(1024)S(1)}, u32[]{:S(2)}, u32[]{:S(2)}) collective-permute-start(f32[6144]{0:T(1024)S(1)} %bitcast.131), channel_id=1, source_target_pairs={{0,4},{4,8},{8,12},{12,16},{16,20},{20,24},{24,28},{1,5},{5,9},{9,... | collective-permute-start | bytes 73736 | tf_op jit(solution)/shard_map/ppermute | solution.py:338
  111.1 1.3 collective-permute-start.5
  112.4 1.7 fusion.56
  114.1 2.7 %collective-permute-done.5 = f32[6144]{0:T(1024)S(1)} collective-permute-done((f32[6144]{0:T(1024)S(1)}, f32[6144]{0:T(1024)S(1)}, u32[]{:S(2)}, u32[]{:S(2)}) %collective-permute-start.5) | collective-permute-done | bytes 24608 | tf_op jit(solution)/shard_map/ppermute | solution.py:339
  117.1 1.3 collective-permute-start.6
  118.5 1.5 collective-permute-start.7
  120.0 0.5 fusion.53
  120.8 0.8 collective-permute-done.7
  121.8 0.5 fusion.4
  122.3 0.4 fusion.13
  122.7 0.4 pad_multiply_fusion.5
  123.0 0.5 fusion.44
  123.6 0.9 fusion.47
  125.1 0.4 pad_multiply_fusion.3
  125.4 0.5 fusion.35
  126.0 0.9 fusion.38
  127.5 0.4 pad_multiply_fusion.1
  127.8 0.5 fusion.26
  128.4 0.9 fusion.29
  129.3 1.5 fusion.7.refs_2_
  130.8 15.3 %lookup.1 = f32[32,2304]{1,0:T(8,128)} custom-call(s32[32]{0:T(128)} %convert_reduce_fusion.1.refs_0_, f32[32,3072]{1,0:T(8,128)} %bitcast.110, f32[3,128,512]{2,1,0:T(8,128)} %fusion.7.refs_2_), custom_call_target="tpu_custom_call" | custom-call | tf_op jit(solution)/shard_map/lookup/pallas_call | solution.py:286
  146.2 1.3 copy.18
  147.4 30.4 %all_to_all.22 = f32[32,1,2304]{2,1,0:T(1,128)S(1)} all-to-all(f32[32,1,2304]{2,1,0:T(1,128)S(1)} %copy.18), channel_id=1, replica_groups=mesh['along'=8,'cross'=4] {'along','cross'}, dimensions={0} | all-to-all | bytes 589824 | tf_op jit(solution)/shard_map/all_to_all | solution.py:434
  177.8 0.7 copy.28
  178.6 9.3 %unpack.1 = f32[3,64,128]{2,1,0:T(8,128)} custom-call(f32[32,2304]{1,0:T(8,128)} %bitcast.112, s32[64,128]{1,0:T(8,128)} %bitcast.119, s32[64,128]{1,0:T(8,128)} %convert_element_type.39.refs_3_.refs_2_), custom_call_target="tpu_custom_call" | custom-call | tf_op jit(solution)/shard_map/unpack/pallas_call | solution.py:325
  (80 shorter events, 4.8 us)
Async XLA Ops:
  0.6 1.0 copy-start.10
  0.6 1.0 copy-start.8
  0.7 1.0 copy-start.7
  0.7 7.4 %copy-start.11 = (s32[4,16,9]{1,0,2:T(4,128)S(1)}, s32[4,16,9]{1,0,2:T(4,128)}, u32[]{:S(2)}) copy-start(s32[4,16,9]{1,0,2:T(4,128)} %param.11) | copy-start | bytes 6916
  0.7 7.5 %copy-start.9 = (s32[1,1,8192,1]{2,3,1,0:T(1,128)S(1)}, s32[1,1,8192,1]{2,3,1,0:T(1,128)}, u32[]{:S(2)}) copy-start(s32[1,1,8192,1]{2,3,1,0:T(1,128)} %param.12) | copy-start | bytes 98308
  1.7 11.3 %copy-start = (f32[3,128,512]{2,1,0:T(8,128)S(1)}, f32[3,128,512]{2,1,0:T(8,128)}, u32[]{:S(2)}) copy-start(f32[3,128,512]{2,1,0:T(8,128)} %param.14) | copy-start | bytes 2359300
  1.7 11.3 %copy-start.2 = (f32[128,512]{1,0:T(8,128)S(1)}, f32[128,512]{1,0:T(8,128)}, u32[]{:S(2)}) copy-start(f32[128,512]{1,0:T(8,128)} %param.15) | copy-start | bytes 786436
  1.7 7.4 %collective-permute-start = (f32[18432]{0:T(1024)S(1)}, f32[18432]{0:T(1024)S(1)}, u32[]{:S(2)}, u32[]{:S(2)}) collective-permute-start(f32[18432]{0:T(1024)S(1)} %pad_maximum_fusion.12), channel_id=1, source_target_pairs={{0,4},{4,8},{8,12},{12,16},{16,20},{20,24},{24,28},{1,5},{5,9},{9,... | collective-permute-start | bytes 221192 | tf_op jit(solution)/shard_map/ppermute | solution.py:338
  6.8 6.2 %collective-permute-start.1 = (f32[18432]{0:T(1024)S(1)}, f32[18432]{0:T(1024)S(1)}, u32[]{:S(2)}, u32[]{:S(2)}) collective-permute-start(f32[18432]{0:T(1024)S(1)} %pad_maximum_fusion.13), channel_id=1, source_target_pairs={{4,0},{8,4},{12,8},{16,12},{20,16},{24,20},{28,24},{5,1},{9,5},{13... | collective-permute-start | bytes 221192 | tf_op jit(solution)/shard_map/ppermute | solution.py:339
  13.5 4.3 %collective-permute-start.2 = (f32[6016]{0:T(1024)S(1)}, f32[6016]{0:T(1024)S(1)}, u32[]{:S(2)}, u32[]{:S(2)}) collective-permute-start(f32[6016]{0:T(1024)S(1)} %pad_maximum_fusion.18), channel_id=1, source_target_pairs={{0,1},{1,2},{2,3},{4,5},{5,6},{6,7},{8,9},{9,10},{10,11},{12,13},{... | collective-permute-start | bytes 72200 | tf_op jit(solution)/shard_map/ppermute | solution.py:338
  15.0 4.8 %collective-permute-start.3 = (f32[6016]{0:T(1024)S(1)}, f32[6016]{0:T(1024)S(1)}, u32[]{:S(2)}, u32[]{:S(2)}) collective-permute-start(f32[6016]{0:T(1024)S(1)} %pad_maximum_fusion.19), channel_id=1, source_target_pairs={{1,0},{2,1},{3,2},{5,4},{6,5},{7,6},{9,8},{10,9},{11,10},{13,12},{... | collective-permute-start | bytes 72200 | tf_op jit(solution)/shard_map/ppermute | solution.py:339
  54.1 20.4 %all-to-all-start = ((f32[32,1,3072]{2,1,0:T(1,128)}), f32[32,1,3072]{2,1,0:T(1,128)}, u32[]{:S(2)}, u32[]{:S(2)}) async-start(f32[32,1,3072]{2,1,0:T(1,128)} %copy.17), calls=%async_computation | async-start | bytes 786432 | tf_op jit(solution)/shard_map/all_to_all | solution.py:412
  74.4 37.9 %copy-start.4 = (f32[138,522]{1,0:T(8,128)S(1)}, f32[138,522]{1,0:T(8,128)}, u32[]{:S(2)}) copy-start(f32[138,522]{1,0:T(8,128)} %get-tuple-element.18) | copy-start | bytes 864436
  75.6 0.8 copy-start.3
  95.4 18.6 %collective-permute-start.4 = (f32[6144]{0:T(1024)S(1)}, f32[6144]{0:T(1024)S(1)}, u32[]{:S(2)}, u32[]{:S(2)}) collective-permute-start(f32[6144]{0:T(1024)S(1)} %bitcast.131), channel_id=1, source_target_pairs={{0,4},{4,8},{8,12},{12,16},{16,20},{20,24},{24,28},{1,5},{5,9},{9,... | collective-permute-start | bytes 73736 | tf_op jit(solution)/shard_map/ppermute | solution.py:338
  111.1 5.7 %collective-permute-start.5 = (f32[6144]{0:T(1024)S(1)}, f32[6144]{0:T(1024)S(1)}, u32[]{:S(2)}, u32[]{:S(2)}) collective-permute-start(f32[6144]{0:T(1024)S(1)} %bitcast.132), channel_id=1, source_target_pairs={{4,0},{8,4},{12,8},{16,12},{20,16},{24,20},{28,24},{5,1},{9,5},{13... | collective-permute-start | bytes 73736 | tf_op jit(solution)/shard_map/ppermute | solution.py:339
  112.4 4.4 %copy-start.1 = (f32[3,128,512]{2,1,0:T(8,128)S(1)}, f32[3,128,512]{2,1,0:T(8,128)}, u32[]{:S(2)}) copy-start(f32[3,128,512]{2,1,0:T(8,128)} %deposit.1) | copy-start | bytes 2359300
  117.1 3.5 %collective-permute-start.6 = (f32[1632]{0:T(1024)S(1)}, f32[1632]{0:T(1024)S(1)}, u32[]{:S(2)}, u32[]{:S(2)}) collective-permute-start(f32[1632]{0:T(1024)S(1)} %reshape.190), channel_id=1, source_target_pairs={{0,1},{1,2},{2,3},{4,5},{5,6},{6,7},{8,9},{9,10},{10,11},{12,13},{... | collective-permute-start | bytes 19592 | tf_op jit(solution)/shard_map/ppermute | solution.py:338
  118.5 3.1 %collective-permute-start.7 = (f32[1632]{0:T(1024)S(1)}, f32[1632]{0:T(1024)S(1)}, u32[]{:S(2)}, u32[]{:S(2)}) collective-permute-start(f32[1632]{0:T(1024)S(1)} %reshape.192), channel_id=1, source_target_pairs={{1,0},{2,1},{3,2},{5,4},{6,5},{7,6},{9,8},{10,9},{11,10},{13,12},{... | collective-permute-start | bytes 19592 | tf_op jit(solution)/shard_map/ppermute | solution.py:339
  120.0 1.8 copy-start.5
  128.4 1.0 copy-start.6

commit v2 on v1

v2 whole, which is shorter than its diff:
```python
import math

import jax
import jax.numpy as jnp
from jax import lax
from jax.experimental import pallas as pl
from jax.experimental.pallas import tpu as pltpu
from jax.sharding import PartitionSpec as P

SUBSTEPS = 4
LANES = 128

courant = 0.4
kernel_width = 1.0
LOG2E = math.log2(math.e) / kernel_width

VMEM_LIMIT = 60 * 1024 * 1024


def split(values):
    high = values.astype(jnp.bfloat16).astype(jnp.float32)
    return high, values - high


def vmem():
    return pl.BlockSpec(memory_space=pltpu.MemorySpace.VMEM)


def smem():
    return pl.BlockSpec(memory_space=pltpu.MemorySpace.SMEM)


def one_hot(index, count):
    size = math.gcd(LANES, count)
    rows = lax.broadcasted_iota(jnp.int32, (size, index.shape[1]), 0).astype(jnp.float32).astype(jnp.bfloat16)
    parts = []
    for first in range(0, count, size):
        here = index - first
        here = jnp.where((here >= 0.0) & (here < size), here, -1.0).astype(jnp.bfloat16)
        parts.append(jnp.where(here == rows, jnp.bfloat16(1), jnp.bfloat16(0)))
    return parts[0] if len(parts) == 1 else jnp.concatenate(parts, axis=0)


def one_hot_t(index, count):
    upper = jnp.floor(index * (1.0 / LANES))
    code = LANES + index - LANES * upper
    for n in range(1, count // LANES):
        code = jnp.where(upper >= n, 2.0 * code, code)
    code = jnp.broadcast_to(code.astype(jnp.bfloat16), (LANES, LANES)).T
    lane = (LANES + lax.broadcasted_iota(jnp.int32, (LANES, LANES), 1)).astype(jnp.float32)
    return jnp.concatenate(
        [
            jnp.where(code == (lane * 2.0**n).astype(jnp.bfloat16), jnp.bfloat16(1), jnp.bfloat16(0))
            for n in range(count // LANES)
        ],
        axis=1,
    )


def is_row(index, count):
    rows = lax.broadcasted_iota(jnp.int32, (count, index.shape[1]), 0).astype(jnp.float32).astype(jnp.bfloat16)
    return jnp.where((index >= 0.0) & (index < count), index, -1.0).astype(jnp.bfloat16) == rows


def columns_of(row):
    return jnp.broadcast_to(row, (LANES, row.shape[1])).T


def sph_kernel(present_ref, pad_ref, density_ref, source_ref, uv_ref, carry_ref, col_ref, acc_ref, sums_ref):
    _, rows2, cols2, size = pad_ref.shape
    rows, cols = rows2 - 2, cols2 - 2
    tiles = rows * cols
    x, y, vx, vy, m = [pad_ref[k] for k in range(5)]
    for d in range(3):
        uv_ref[d] = (2.0 * LOG2E) * (x + (d - 1.0))
        uv_ref[3 + d] = (2.0 * LOG2E) * (y + (d - 1.0))
    gx = [jnp.exp2(-LOG2E * (x + (d - 1.0)) * (x + (d - 1.0))) for d in range(3)]
    gy = [jnp.exp2(-LOG2E * (y + (d - 1.0)) * (y + (d - 1.0))) for d in range(3)]
    for di in range(3):
        for dj in range(3):
            g = gx[di] * gy[dj] * m
            carry_ref[3 * (3 * di + dj)] = g
            carry_ref[3 * (3 * di + dj) + 1] = g * vx
            carry_ref[3 * (3 * di + dj) + 2] = g * vy

    def prepare(t, slot):
        i, j = t // cols, t % cols
        for k in range(2):
            col_ref[slot, k] = columns_of(pad_ref[k, i + 1, pl.ds(j + 1, 1), :])

    def finish(t, slot):
        for k in range(3):
            sums_ref[k, pl.ds(t, 1), :] = jnp.sum(acc_ref[slot, k].T, axis=0, keepdims=True)

    def compute(t, slot):
        i, j = t // cols, t % cols
        half = size // 2
        for h in range(2):
            xa = col_ref[slot, 0, h * half : (h + 1) * half, :]
            ya = col_ref[slot, 1, h * half : (h + 1) * half, :]
            acc = [jnp.zeros((half, size), jnp.float32) for _ in range(3)]
            for w in range(9):
                di, dj = w // 3, w % 3
                there = present_ref[t * 9 + w]
                u = uv_ref[di, i + di, pl.ds(j + dj, 1), :]
                v = uv_ref[3 + dj, i + di, pl.ds(j + dj, 1), :]
                weight = jnp.exp2(xa * u + ya * v)
                for k in range(3):
                    acc[k] = acc[k] + weight * (carry_ref[3 * w + k, i + di, pl.ds(j + dj, 1), :] * there)
            for k in range(3):
                acc_ref[slot, k, h * half : (h + 1) * half, :] = acc[k]

    prepare(0, 0)

    def step(p, _):
        for slot in range(2):
            t = 2 * p + slot
            prepare(jnp.minimum(t + 1, tiles - 1), 1 - slot)
            finish(jnp.maximum(t - 1, 0), 1 - slot)
            compute(t, slot)
        return 0

    lax.fori_loop(0, tiles // 2, step, 0)
    finish(tiles - 1, (tiles - 1) % 2)

    for i in range(rows):
        own = pad_ref[:, i + 1, 1 : cols + 1, :]
        outer = jnp.exp2(-LOG2E * (own[0] * own[0] + own[1] * own[1]))
        s0 = outer * sums_ref[0, i * cols : (i + 1) * cols, :]
        s1 = outer * sums_ref[1, i * cols : (i + 1) * cols, :]
        s2 = outer * sums_ref[2, i * cols : (i + 1) * cols, :]
        density = s0 / size
        volume = own[4] / density
        density_ref[i] = density
        source_ref[0, i * cols : (i + 1) * cols, :] = volume
        source_ref[1, i * cols : (i + 1) * cols, :] = volume * (s1 / s0)
        source_ref[2, i * cols : (i + 1) * cols, :] = volume * (s2 / s0)


def sph(padded, present):
    _, rows2, cols2, size = padded.shape
    rows, cols = rows2 - 2, cols2 - 2
    return pl.pallas_call(
        sph_kernel,
        out_shape=(
            jax.ShapeDtypeStruct((rows, cols, size), jnp.float32),
            jax.ShapeDtypeStruct((3, rows * cols, size), jnp.float32),
        ),
        in_specs=[smem(), vmem()],
        out_specs=(vmem(), vmem()),
        scratch_shapes=[
            pltpu.VMEM((6, rows2, cols2, size), jnp.float32),
            pltpu.VMEM((27, rows2, cols2, size), jnp.float32),
            pltpu.VMEM((2, 2, size, size), jnp.float32),
            pltpu.VMEM((2, 3, size, size), jnp.float32),
            pltpu.VMEM((3, rows * cols, size), jnp.float32),
        ],
        compiler_params=pltpu.CompilerParams(vmem_limit_bytes=VMEM_LIMIT),
        name="sph",
    )(present, padded)


def pack_kernel(source_ref, cell_ref, dest_ref, rank_ref, out_ref, acc_ref, *, group):
    tiles, size = cell_ref.shape
    devices = out_ref.shape[0]
    capacity = acc_ref.shape[1]
    acc_ref[...] = jnp.zeros_like(acc_ref)

    def work(b, _):
        lefts, rights = [], []
        for s in range(group):
            t = b * group + s
            cell = cell_ref[pl.ds(t, 1), :].astype(jnp.float32)
            upper = jnp.floor(cell * (1.0 / 256.0))
            values = [upper, cell - 256.0 * upper]
            for k in range(3):
                values.extend(split(source_ref[k, pl.ds(t, 1), :]))
            mine = is_row(dest_ref[pl.ds(t, 1), :].astype(jnp.float32), devices)
            lefts.append(
                jnp.concatenate(
                    [jnp.where(mine, value.astype(jnp.bfloat16), jnp.bfloat16(0)) for value in values], axis=0
                )
            )
            rights.append(one_hot(rank_ref[pl.ds(t, 1), :].astype(jnp.float32), capacity))
        acc_ref[...] += lax.dot_general(
            jnp.concatenate(lefts, axis=1),
            jnp.concatenate(rights, axis=1),
            (((1,), (1,)), ((), ())),
            preferred_element_type=jnp.float32,
        )
        return 0

    lax.fori_loop(0, tiles // group, work, 0)

    def part(c):
        return acc_ref[c * devices : (c + 1) * devices, :]

    outs = [256.0 * part(0) + part(1)] + [part(2 + 2 * k) + part(3 + 2 * k) for k in range(3)]
    blocks = capacity // LANES
    for k, out in enumerate(outs):
        for b in range(blocks):
            out_ref[:, k * blocks + b, :] = out[:, b * LANES : (b + 1) * LANES]


def pack(source, cell, dest, rank, devices, capacity):
    tiles, size = cell.shape
    group = math.gcd(16, tiles)
    return pl.pallas_call(
        lambda *refs: pack_kernel(*refs, group=group),
        out_shape=jax.ShapeDtypeStruct((devices, 4 * capacity // LANES, LANES), jnp.float32),
        in_specs=[vmem()] * 4,
        out_specs=vmem(),
        scratch_shapes=[pltpu.VMEM((8 * devices, capacity), jnp.float32)],
        compiler_params=pltpu.CompilerParams(vmem_limit_bytes=VMEM_LIMIT),
        name="pack",
    )(source, cell, dest, rank)


def row_and_col(cell, cells_cross):
    row = jnp.floor((cell + 0.5) * (1.0 / cells_cross))
    return row, cell - cells_cross * row


GROUP = 16


def list_blocks(start_ref, amount_ref, block_ref, bound_ref, *, senders, bins, blocks):
    total = 0
    together = math.gcd(8, senders)
    for q in range(bins):

        def some(g, total):
            for n in range(together):
                s = g * together + n
                first = 4 * blocks * s + start_ref[s * bins + q]
                for b in range(blocks):
                    block_ref[total + b] = first + b
                total = total + amount_ref[s * bins + q]
            return total

        total = lax.fori_loop(0, senders // together, some, total)
        for b in range(GROUP):
            block_ref[total + b] = -1
        total = (total + GROUP - 1) // GROUP * GROUP
        bound_ref[q] = total // GROUP
    for b in range(3 * GROUP):
        block_ref[total + b] = -1


def list_sizes(senders, bins, blocks):
    return senders * (blocks + bins) + (bins + 4) * GROUP, bins


def bin_of(group, bound_ref, bins):
    q = 0
    for n in range(bins - 1):
        q = q + (group >= bound_ref[n]).astype(jnp.int32)
    return q


def by_group(bound_ref, bins, work):
    def pair(p, _):
        for n in range(2):
            work(2 * p + n)
        return 0

    lax.fori_loop(0, (bound_ref[bins - 1] + 1) // 2, pair, 0)


def block_cells(in_ref, row, base, cells_cross):
    there = jnp.maximum(row, 0)
    row_of, col_of = row_and_col(in_ref[pl.ds(there, 1), :], cells_cross)
    return there, row_of - jnp.where(row < 0, 1 << 20, base).astype(jnp.float32), col_of


def deposit_kernel(start_ref, amount_ref, in_ref, out_ref, block_ref, bound_ref, *, senders, bins, blocks):
    _, cells_along, cells_cross = out_ref.shape
    height = cells_along // bins
    list_blocks(start_ref, amount_ref, block_ref, bound_ref, senders=senders, bins=bins, blocks=blocks)
    out_ref[...] = jnp.zeros_like(out_ref)

    def work(group):
        base = bin_of(group, bound_ref, bins) * height
        lefts, rights = [], []
        for b in range(GROUP):
            row, row_of, col_of = block_cells(in_ref, block_ref[group * GROUP + b], base, cells_cross)
            mine = is_row(row_of, height)
            values = [part for k in range(3) for part in split(in_ref[pl.ds(row + (k + 1) * blocks, 1), :])]
            lefts.append(
                jnp.concatenate(
                    [jnp.where(mine, value.astype(jnp.bfloat16), jnp.bfloat16(0)) for value in values], axis=0
                )
            )
            rights.append(one_hot_t(col_of, cells_cross))
        both = jnp.dot(
            jnp.concatenate(lefts, axis=1), jnp.concatenate(rights, axis=0), preferred_element_type=jnp.float32
        )
        for k in range(3):
            part = both[2 * k * height : (2 * k + 1) * height] + both[(2 * k + 1) * height : (2 * k + 2) * height]
            out_ref[k, pl.ds(pl.multiple_of(base, height), height), :] += part

    by_group(bound_ref, bins, work)


def deposit(incoming, starts, amounts, bins, cells_along, cells_cross):
    senders = incoming.shape[0]
    blocks = incoming.shape[1] // 4
    size, bounds = list_sizes(senders, bins, blocks)
    return pl.pallas_call(
        lambda *refs: deposit_kernel(*refs, senders=senders, bins=bins, blocks=blocks),
        out_shape=(
            jax.ShapeDtypeStruct((3, cells_along, cells_cross), jnp.float32),
            jax.ShapeDtypeStruct((size,), jnp.int32),
            jax.ShapeDtypeStruct((bounds,), jnp.int32),
        ),
        in_specs=[smem(), smem(), vmem()],
        out_specs=(vmem(), smem(), smem()),
        compiler_params=pltpu.CompilerParams(vmem_limit_bytes=VMEM_LIMIT),
        name="deposit",
    )(starts, amounts, incoming.reshape(-1, LANES))


def substeps(edge_ref, water_ref, source_ref, state_ref, margin):
    _, cells_along, cells_cross = state_ref.shape
    _, height, width = water_ref.shape
    rows = lax.broadcasted_iota(jnp.int32, (height, width), 0)
    cols = lax.broadcasted_iota(jnp.int32, (height, width), 1)
    inside = (rows >= edge_ref[0]) & (rows < edge_ref[1]) & (cols >= edge_ref[2]) & (cols < edge_ref[3])

    def along(field):
        return pltpu.roll(field, height - 1, 0), pltpu.roll(field, 1, 0)

    def cross(field):
        return pltpu.roll(field, width - 1, 1), pltpu.roll(field, 1, 1)

    depth = water_ref[3]
    elevation, speed_x, speed_y = water_ref[0], water_ref[1], water_ref[2]
    for _ in range(SUBSTEPS):
        east, west = along(elevation)
        north, south = cross(elevation)
        flux_east, flux_west = along(depth * speed_x)
        flux_north, flux_south = cross(depth * speed_y)
        around = [sum(along(f) + cross(f)) for f in (speed_x, speed_y)]
        flow = flux_east - flux_west + flux_north - flux_south
        following = (
            0.25 * (east + west + north + south) - 0.5 * courant * flow,
            0.25 * around[0] - 0.5 * courant * (east - west),
            0.25 * around[1] - 0.5 * courant * (north - south),
        )
        elevation, speed_x, speed_y = [
            jnp.where(inside, value + source_ref[k], 0.0) for k, value in enumerate(following)
        ]
    for k, field in enumerate((elevation, speed_x, speed_y)):
        field = pltpu.roll(pltpu.roll(field, height - margin, 0), width - margin, 1)
        state_ref[k] = field[:cells_along, :cells_cross]


def lookup_kernel(
    block_ref, bound_ref, edge_ref, in_ref, water_ref, source_ref, out_ref, state_ref, left_ref, *, bins, blocks, margin
):
    _, cells_along, cells_cross = state_ref.shape
    height = cells_along // bins
    substeps(edge_ref, water_ref, source_ref, state_ref, margin)
    for k in range(3):
        for h, value in enumerate(split(state_ref[k])):
            q = 2 * k + h
            for n in range(bins):
                left_ref[n, q * height : (q + 1) * height, :] = value[n * height : (n + 1) * height].astype(jnp.bfloat16)
    out_ref[...] = jnp.zeros_like(out_ref)

    def work(group):
        q = bin_of(group, bound_ref, bins)
        right = jnp.concatenate(
            [
                one_hot(block_cells(in_ref, block_ref[group * GROUP + b], 0, cells_cross)[2], cells_cross)
                for b in range(GROUP)
            ],
            axis=1,
        )
        every = jnp.dot(left_ref[q], right, preferred_element_type=jnp.float32)
        for b in range(GROUP):
            at = slice(b * LANES, (b + 1) * LANES)
            row, row_of, _ = block_cells(in_ref, block_ref[group * GROUP + b], q * height, cells_cross)
            mine = row_of == lax.broadcasted_iota(jnp.int32, (height, LANES), 0).astype(jnp.float32)
            for k in range(3):
                both = every[2 * k * height : (2 * k + 1) * height, at] + every[(2 * k + 1) * height : (2 * k + 2) * height, at]
                found = jnp.sum(jnp.where(mine, both, 0.0), axis=0, keepdims=True)
                out_ref[pl.ds(row - row // (4 * blocks) * blocks + k * blocks, 1), :] += found

    by_group(bound_ref, bins, work)


def lookup(incoming, block_list, bounds, edges, water, source, bins, margin, cells_along, cells_cross):
    senders, rows, _ = incoming.shape
    return pl.pallas_call(
        lambda *refs: lookup_kernel(*refs, bins=bins, blocks=rows // 4, margin=margin),
        out_shape=(
            jax.ShapeDtypeStruct((senders * rows // 4 * 3, LANES), jnp.float32),
            jax.ShapeDtypeStruct((3, cells_along, cells_cross), jnp.float32),
        ),
        in_specs=[smem()] * 3 + [vmem()] * 3,
        out_specs=(vmem(), vmem()),
        scratch_shapes=[pltpu.VMEM((bins, 6 * cells_along // bins, cells_cross), jnp.bfloat16)],
        compiler_params=pltpu.CompilerParams(vmem_limit_bytes=VMEM_LIMIT),
        name="lookup",
    )(block_list, bounds, edges, incoming.reshape(-1, LANES), water, source)


def unpack_kernel(in_ref, dest_ref, rank_ref, out_ref, left_ref, *, capacity, group):
    tiles, size = dest_ref.shape
    blocks = capacity // LANES
    devices = in_ref.shape[0] // (3 * blocks)
    for k in range(3):
        for b in range(blocks):
            for h, value in enumerate(split(in_ref[pl.ds(k * blocks + b, devices, stride=3 * blocks), :])):
                q = 2 * k + h
                left_ref[q * devices : (q + 1) * devices, b * LANES : (b + 1) * LANES] = value.astype(jnp.bfloat16)

    def step(b, _):
        right = jnp.concatenate(
            [one_hot(rank_ref[pl.ds(b * group + s, 1), :].astype(jnp.float32), capacity) for s in range(group)], axis=1
        )
        every = jnp.dot(left_ref[...], right, preferred_element_type=jnp.float32)
        for s in range(group):
            t = b * group + s
            at = slice(s * size, (s + 1) * size)
            mine = dest_ref[pl.ds(t, 1), :] == lax.broadcasted_iota(jnp.int32, (devices, size), 0)
            for k in range(3):
                both = every[2 * k * devices : (2 * k + 1) * devices, at]
                both = both + every[(2 * k + 1) * devices : (2 * k + 2) * devices, at]
                out_ref[k, pl.ds(t, 1), :] = jnp.sum(jnp.where(mine, both, 0.0), axis=0, keepdims=True)
        return 0

    lax.fori_loop(0, tiles // group, step, 0)


def unpack(returned, dest, rank, capacity):
    tiles, size = dest.shape
    devices = returned.shape[0] * LANES // (3 * capacity)
    group = math.gcd(16, tiles)
    return pl.pallas_call(
        lambda *refs: unpack_kernel(*refs, capacity=capacity, group=group),
        out_shape=jax.ShapeDtypeStruct((3, tiles, size), jnp.float32),
        in_specs=[vmem()] * 3,
        out_specs=vmem(),
        scratch_shapes=[pltpu.VMEM((6 * devices, capacity), jnp.bfloat16)],
        compiler_params=pltpu.CompilerParams(vmem_limit_bytes=VMEM_LIMIT),
        name="unpack",
    )(returned, dest, rank)


def swap(axis, to_next, to_previous):
    count = lax.axis_size(axis)
    before = lax.ppermute(to_next, axis, [(i, i + 1) for i in range(count - 1)])
    after = lax.ppermute(to_previous, axis, [(i + 1, i) for i in range(count - 1)])
    return before, after


def padded_together(fields):
    arrays = [array for array, _, _ in fields]
    for step, axis in enumerate(("along", "cross")):
        heads, tails = [], []
        for array, (_, dims, width) in zip(arrays, fields):
            dim = dims[step]
            heads.append(lax.slice_in_dim(array, 0, width, axis=dim))
            tails.append(lax.slice_in_dim(array, array.shape[dim] - width, array.shape[dim], axis=dim))
        flat = lambda parts: jnp.concatenate([part.reshape(-1) for part in parts])
        before, after = swap(axis, flat(tails), flat(heads))
        start, grown = 0, []
        for array, head, (_, dims, _) in zip(arrays, heads, fields):
            rims = [rim[start : start + head.size].reshape(head.shape) for rim in (before, after)]
            start += head.size
            grown.append(jnp.concatenate([rims[0], array, rims[1]], axis=dims[step]))
        arrays = grown
    return arrays


def slot_ranks(key, destination, devices, bins):
    groups, block = key.shape
    onehot = (key[:, :, None] == jnp.arange(devices * bins, dtype=jnp.int32)).astype(jnp.bfloat16)
    lower = (jnp.arange(block)[:, None] > jnp.arange(block)[None, :]).astype(jnp.bfloat16)
    earlier = jnp.einsum("ij,bjd->bid", lower, onehot, preferred_element_type=jnp.float32)
    counts = jnp.sum(onehot.astype(jnp.float32), axis=1)
    totals = jnp.sum(counts, axis=0).reshape(devices, bins)
    first = (jnp.cumsum(totals, axis=1) - totals).reshape(-1)
    before = jnp.cumsum(counts, axis=0) - counts + first
    return jnp.sum(onehot.astype(jnp.float32) * (earlier + before[:, None, :]), axis=2).astype(jnp.int32)


def shards(offsets, velocity, particle_mass, neighbours, owner_device, target_cell, surface, water_depth):
    _, tiles_along, tiles_cross, tile_size = offsets.shape
    _, cells_along, cells_cross = surface.shape
    along_count = lax.axis_size("along")
    cross_count = lax.axis_size("cross")
    devices = along_count * cross_count
    tiles = tiles_along * tiles_cross
    particles = tiles * tile_size
    capacity = -(-3 * particles // devices // LANES) * LANES
    margin = SUBSTEPS

    stacked = jnp.concatenate([offsets, velocity, particle_mass[None]], axis=0)
    water = jnp.concatenate([surface, water_depth[None]], axis=0)
    padded, wide_water = padded_together([(stacked, (1, 2), 1), (water, (1, 2), margin)])

    destination = owner_device.reshape(tiles, tile_size)
    cell = target_cell.reshape(tiles, tile_size)
    bins = max(1, min(4, LANES // devices))
    rank = slot_ranks(destination * bins + cell // (cells_along * cells_cross // bins), destination, devices, bins)
    present = jnp.any(neighbours[..., :, None] == jnp.arange(9, dtype=jnp.int32), axis=-2).astype(jnp.float32)

    density, sources = sph(padded, present.reshape(-1))
    outgoing = pack(sources, cell, destination, rank, devices, capacity)
    incoming = lax.all_to_all(outgoing, ("along", "cross"), split_axis=0, concat_axis=0, tiled=True)
    blocks = capacity // LANES
    filled = incoming[:, blocks : 2 * blocks] != 0.0
    bin_in = jnp.floor(incoming[:, :blocks] * (bins / (cells_along * cells_cross)))
    counts = jnp.stack([jnp.sum((filled & (bin_in == q)).astype(jnp.int32), axis=(1, 2)) for q in range(bins)], axis=1)
    ends = jnp.cumsum(counts, axis=1)
    starts = (ends - counts) // LANES
    amounts = jnp.where(counts > 0, (ends + LANES - 1) // LANES - starts, 0)
    grid_source, block_list, bounds = deposit(
        incoming, starts.reshape(-1), amounts.reshape(-1), bins, cells_along, cells_cross
    )
    (wide_source,) = padded_together([(grid_source, (1, 2), margin)])

    edges = []
    for axis, length in (("along", cells_along), ("cross", cells_cross)):
        place = lax.axis_index(axis)
        edges.append(jnp.where(place == 0, margin, 0))
        edges.append(jnp.where(place == lax.axis_size(axis) - 1, length + margin, length + 2 * margin))
    to_lanes = [(0, 0), (0, 0), (0, -(cells_cross + 2 * margin) % LANES)]
    looked, water_state = lookup(
        incoming,
        block_list,
        bounds,
        jnp.stack(edges).astype(jnp.int32),
        jnp.pad(wide_water, to_lanes),
        jnp.pad(wide_source, to_lanes),
        bins,
        margin,
        cells_along,
        cells_cross,
    )
    returned = lax.all_to_all(
        looked.reshape(devices, 3 * capacity), ("along", "cross"), split_axis=0, concat_axis=0, tiled=True
    ).reshape(looked.shape)
    feedback = unpack(returned, destination, rank, capacity)
    return water_state, density, feedback.reshape(3, tiles_along, tiles_cross, tile_size)


def solution(mesh):
    in_specs = (
        P(None, "along", "cross", None),
        P(None, "along", "cross", None),
        P("along", "cross", None),
        P("along", "cross", None),
        P("along", "cross", None, None),
        P("along", "cross", None),
        P(None, "along", "cross"),
        P("along", "cross"),
    )
    out_specs = (
        P(None, "along", "cross"),
        P("along", "cross", None),
        P(None, "along", "cross", None),
    )
    return jax.shard_map(shards, mesh=mesh, in_specs=in_specs, out_specs=out_specs, check_vma=False)
```

time: 188 us -> 140 us (0.74); the launches traced: 188 us -> 138 us
  Pallas kernels: 74.1 us -> 54.2 us
  blocking collectives: 30.4 us -> 19.3 us
  starting transfers between devices: 35.7 us -> 25.5 us
  local copies, waits for them, and re-layouts: 11.2 us -> 4.43 us
  other arithmetic: 16 us -> 11.9 us
    all_to_all x1, blocking collectives: 30.4 us -> 19.3 us  [shards(): lax.all_to_all(looked.reshape(devices, 3 * capacity), ('along', 'cross'),...]
    pallas_call x2, Pallas kernels: 33.6 us -> 22.9 us  [the longest x1 13.6 us: lookup(): pl.pallas_call(lambda *refs: lookup_kernel(*refs, bins=bins, blocks=rows...]
    ppermute x4, starting transfers between devices: 23.2 us -> 12.9 us  [swap(): before = lax.ppermute(to_next, axis, [(i, i + 1) for i in range(count - 1)])]
    another operation x9 -> x4, other arithmetic: 6.7 us -> 0.97 us  [the longest x1 0.68 us: shards(): jnp.stack(edges).astype(jnp.int32)]
    mul x8 -> x0, other arithmetic: 4.56 us -> none  [the longest x4 2.32 us: shards(): wide_state = (lax_friedrichs(state_pad, depth_pad) + wide_source) * inside]
    pallas_call x1, Pallas kernels: 9.27 us -> 4.93 us  [unpack(): pl.pallas_call(lambda *refs: unpack_kernel(*refs, capacity=capacity, grou...]
    pallas_call x1, Pallas kernels: 10 us -> 6.04 us  [pack(): pl.pallas_call(lambda *refs: pack_kernel(*refs, group=group), out_shape=j...]
    all_to_all x1, waiting for transfers between devices: 9.34 us -> 13.2 us  [shards(): lax.all_to_all(outgoing, ('along', 'cross'), split_axis=0, concat_axis=0,...]
  transfers between devices with their start and end apart: 9 -> 9, of which waited for: 5 -> 4; matrix products, arithmetic and copies ran while one was open for 5% -> 6% of each run, Pallas kernels for 0% -> 0%
where the time goes in v2:
time: 140 us; the launch traced here: 138 us
  Pallas kernels  54.2 us (39%)
  starting transfers between devices  25.5 us (18%)
  waiting for transfers between devices  19.7 us (14%)
  blocking collectives  19.3 us (14%)
  other arithmetic  11.9 us (8%)
  local copies, waits for them, and re-layouts  4.43 us (3%)
  matrix products  1.69 us (1%)
    pallas_call x1, Pallas kernels, sph(): pl.pallas_call(sph_kernel, out_shape=(jax.ShapeDtypeStruct((rows, cols, s...  20.3 us
    all_to_all x1, blocking collectives, shards(): lax.all_to_all(looked.reshape(devices, 3 * capacity), ('along', 'cross'),...  19.3 us
    pallas_call x1, Pallas kernels, lookup(): pl.pallas_call(lambda *refs: lookup_kernel(*refs, bins=bins, blocks=rows...  13.6 us
    all_to_all x1, waiting for transfers between devices, shards(): lax.all_to_all(outgoing, ('along', 'cross'), split_axis=0, concat_axis=0,...  13.2 us
    ppermute x4, starting transfers between devices, swap(): before = lax.ppermute(to_next, axis, [(i, i + 1) for i in range(count - 1)])  12.9 us
    pallas_call x1, Pallas kernels, deposit(): pl.pallas_call(lambda *refs: deposit_kernel(*refs, senders=senders, bins=...  9.37 us
    all_to_all x1, starting transfers between devices, shards(): lax.all_to_all(outgoing, ('along', 'cross'), split_axis=0, concat_axis=0,...  7.22 us
    ppermute x4, waiting for transfers between devices, swap(): lax.ppermute(to_previous, axis, [(i + 1, i) for i in range(count - 1)])  6.47 us
  transfers between devices with their start and end apart: 9, of which 4 were waited for; matrix products, arithmetic and copies ran while one was open for 6% of the time, Pallas kernels for 0%

profile of v2, /device:TPU:0, one launch (start us, length us, event | category | flops | bytes accessed | tf_op | source)
XLA Modules:
  0.0 137.8 jit_solution(9616309390503366282)
XLA Ops:
  0.7 0.9 maximum_bitcast_fusion
  1.6 0.8 pad_maximum_fusion.12
  2.4 4.9 %collective-permute-start = (f32[18432]{0:T(1024)S(1)}, f32[18432]{0:T(1024)S(1)}, u32[]{:S(2)}, u32[]{:S(2)}) collective-permute-start(f32[18432]{0:T(1024)S(1)} %pad_maximum_fusion.8), channel_id=1, source_target_pairs={{0,4},{4,8},{8,12},{12,16},{16,20},{20,24},{24,28},{1,5},{5,9},{9,... | collective-permute-start | bytes 221192 | tf_op jit(solution)/shard_map/ppermute | solution.py:454
  7.3 1.3 collective-permute-start.1
  8.6 1.3 convert_reduce_fusion
  10.0 0.2 reduce_window_sum.36
  10.2 0.1 reduce_window_sum.37
  10.4 1.7 %fusion = f32[64,128]{1,0:T(8,128)S(1)} fusion(f32[64,128]{1,0:T(8,128)S(1)} %subtract_add_fusion, s32[64,128]{1,0:T(8,128)S(1)} %fusion.21), kind=kOutput, calls=%fused_computation.3 | convolution fusion | flops 275783680 | bytes 98304 | tf_op jit(solution)/shard_map/ij,bjd->bid/dot_general | solution.py:482
  12.2 1.3 collective-permute-done.1
  13.6 0.2 pad_maximum_fusion.4
  13.8 0.2 reshape.209
  14.1 1.3 collective-permute-start.2
  15.4 0.2 reshape.212
  15.6 1.3 collective-permute-start.3
  17.1 0.7 reshape.230.present_ref
  17.8 0.6 convert_element_type.38.refs_3_.refs_2_
  18.5 2.0 %collective-permute-done.3 = f32[6016]{0:T(1024)S(1)} collective-permute-done((f32[6016]{0:T(1024)S(1)}, f32[6016]{0:T(1024)S(1)}, u32[]{:S(2)}, u32[]{:S(2)}) %collective-permute-start.3) | collective-permute-done | bytes 24096 | tf_op jit(solution)/shard_map/ppermute | solution.py:455
  20.5 0.8 pad_maximum_fusion.pad_ref
  21.3 20.3 %sph.1 = (f32[4,16,128]{2,1,0:T(8,128)}, f32[3,64,128]{2,1,0:T(8,128)}) custom-call(f32[576]{0:T(1024)} %reshape.230.present_ref, f32[5,6,18,128]{3,2,1,0:T(8,128)} %pad_maximum_fusion.pad_ref), custom_call_target="tpu_custom_call" | custom-call | tf_op jit(solution)/shard_map/sph/pallas_call | solution.py:143
  41.6 6.0 %pack.1 = f32[32,24,128]{2,1,0:T(8,128)} custom-call(f32[3,64,128]{2,1,0:T(8,128)} %get-tuple-element.10.refs_0_, s32[64,128]{1,0:T(8,128)} %bitcast.56, s32[64,128]{1,0:T(8,128)} %bitcast.47, s32[64,128]{1,0:T(8,128)} %convert_element_type.38.refs_3_.refs_2_), custom_call_target="tpu_custom_call" | custom-call | tf_op jit(solution)/shard_map/pack/pallas_call | solution.py:208
  47.6 7.2 %all-to-all-start = ((f32[32,24,128]{2,1,0:T(8,128)}), f32[32,24,128]{2,1,0:T(8,128)S(1)}, u32[]{:S(2)}, u32[]{:S(2)}) async-start(f32[32,24,128]{2,1,0:T(8,128)} %pack.1), calls=%async_computation | async-start | bytes 786432 | tf_op jit(solution)/shard_map/all_to_all | solution.py:513
  54.8 13.2 %all-to-all-done = f32[32,24,128]{2,1,0:T(8,128)S(1)} async-done(((f32[32,24,128]{2,1,0:T(8,128)}), f32[32,24,128]{2,1,0:T(8,128)S(1)}, u32[]{:S(2)}, u32[]{:S(2)}) %all-to-all-start) | async-done | bytes 393248 | tf_op jit(solution)/shard_map/all_to_all | solution.py:513
  68.1 2.4 %convert_reduce_fusion.5 = (s32[32]{0:T(128)S(1)}, s32[32]{0:T(128)S(1)}, s32[32]{0:T(128)S(1)}, s32[32]{0:T(128)S(1)}) fusion(f32[32,24,128]{2,1,0:T(8,128)S(1)} %all-to-all-done), kind=kLoop, calls=%fused_computation.42 | loop fusion | flops 466816 | bytes 197120 | tf_op jit(solution)/shard_map/reduce_sum | solution.py:517
  70.6 0.1 sub.52
  70.8 0.1 sub.55
  70.9 0.1 copy.26
  71.0 0.1 gt.25
  71.1 0.6 subtract_select_fusion
  71.7 9.4 %deposit.1 = (f32[3,128,512]{2,1,0:T(8,128)}, s32[448]{0:T(512)}, s32[4]{0:T(128)}) custom-call(s32[128]{0:T(128)} %get-tuple-element.26.refs_0_, s32[128]{0:T(128)} %get-tuple-element.25.refs_1_, f32[768,128]{1,0:T(8,128)} %bitcast.37), custom_call_target="tpu_custom_call" | custom-call | tf_op jit(solution)/shard_map/deposit/pallas_call | solution.py:309
  81.1 0.9 slice_bitcast_fusion.1
  82.0 5.0 %collective-permute-start.4 = (f32[6144]{0:T(1024)S(1)}, f32[6144]{0:T(1024)S(1)}, u32[]{:S(2)}, u32[]{:S(2)}) collective-permute-start(f32[6144]{0:T(1024)S(1)} %bitcast.61), channel_id=1, source_target_pairs={{0,4},{4,8},{8,12},{12,16},{16,20},{20,24},{24,28},{1,5},{5,9},{9,... | collective-permute-start | bytes 73736 | tf_op jit(solution)/shard_map/ppermute | solution.py:454
  87.0 1.3 collective-permute-start.5
  88.3 0.7 pad_add_fusion.1.refs_2_
  89.0 0.3 reshape.218
  89.3 0.3 reshape.219
  89.6 3.2 %collective-permute-done.5 = f32[6144]{0:T(1024)S(1)} collective-permute-done((f32[6144]{0:T(1024)S(1)}, f32[6144]{0:T(1024)S(1)}, u32[]{:S(2)}, u32[]{:S(2)}) %collective-permute-start.5) | collective-permute-done | bytes 24608 | tf_op jit(solution)/shard_map/ppermute | solution.py:455
  92.8 0.1 pad_maximum_fusion.7
  92.9 0.1 reshape.224
  93.1 1.8 %collective-permute-start.6 = (f32[1632]{0:T(1024)S(1)}, f32[1632]{0:T(1024)S(1)}, u32[]{:S(2)}, u32[]{:S(2)}) collective-permute-start(f32[1632]{0:T(1024)S(1)} %reshape.224), channel_id=1, source_target_pairs={{0,1},{1,2},{2,3},{4,5},{5,6},{6,7},{8,9},{9,10},{10,11},{12,13},{... | collective-permute-start | bytes 19592 | tf_op jit(solution)/shard_map/ppermute | solution.py:454
  94.9 0.1 reshape.226
  95.0 1.5 %collective-permute-start.7 = (f32[1632]{0:T(1024)S(1)}, f32[1632]{0:T(1024)S(1)}, u32[]{:S(2)}, u32[]{:S(2)}) collective-permute-start(f32[1632]{0:T(1024)S(1)} %reshape.226), channel_id=1, source_target_pairs={{1,0},{2,1},{3,2},{5,4},{6,5},{7,6},{9,8},{10,9},{11,10},{13,12},{... | collective-permute-start | bytes 19592 | tf_op jit(solution)/shard_map/ppermute | solution.py:455
  96.5 1.7 %select_maximum_fusion.refs_4_ = f32[4,136,640]{2,1,0:T(8,128)} fusion(f32[4,136,4]{2,1,0:T(8,128)S(1)} %reshape.219, f32[4,136,4]{2,1,0:T(8,128)S(1)} %reshape.218, f32[4,4,512]{2,1,0:T(4,128)S(1)} %slice.118, f32[4,4,512]{2,1,0:T(4,128)S(1)} %slice.116, f32[1,128,512]{2,1,0:T(8,128)S(1)} %bitcast.41, f32[3,128,512]{2,1,0:T(8,128)S(1)} %copy-done), kind=kLoop, calls=%fused_computation.8 | loop fusion | flops 4177920 | bytes 2524160 | tf_op jit(solution)/shard_map/concatenate | solution.py:473
  98.2 0.2 reshape.225
  98.4 0.2 reshape.227
  98.7 1.4 %select_maximum_fusion.2.refs_5_ = f32[3,136,640]{2,1,0:T(8,128)} fusion(f32[3,136,4]{2,1,0:T(8,128)S(1)} %reshape.227, f32[3,136,4]{2,1,0:T(8,128)S(1)} %reshape.225, f32[3,4,512]{2,1,0:T(4,128)S(1)} %reshape.223, f32[3,128,512]{2,1,0:T(8,128)S(1)} %copy-done.2, f32[3,4,512]{2,1,0:T(4,128)S(1)} %reshape.221), kind=kLoop, calls=%fused_computation.18 | loop fusion | flops 2611200 | bytes 1893120 | tf_op jit(solution)/shard_map/concatenate | solution.py:473
  100.1 13.6 %lookup.1 = (f32[576,128]{1,0:T(8,128)}, f32[3,128,512]{2,1,0:T(8,128)}) custom-call(s32[448]{0:T(512)} %get-tuple-element.11.refs_0_, s32[4]{0:T(128)} %get-tuple-element.12.refs_1_, s32[4]{0:T(128)} %pad_add_fusion.1.refs_2_, f32[768,128]{1,0:T(8,128)} %bitcast.38, f32[4,136,640]{2,1,0:T(8,128)} %select_maximum_fusion.refs_4_, ...), custom_call_target="tpu_custom_call" | custom-call | tf_op jit(solution)/shard_map/lookup/pallas_call | solution.py:395
  113.6 19.3 %all_to_all.14 = f32[32,1,2304]{2,1,0:T(1,128)} all-to-all(f32[32,1,2304]{2,1,0:T(1,128)} %bitcast.53), channel_id=1, replica_groups=mesh['along'=8,'cross'=4] {'along','cross'}, dimensions={0} | all-to-all | bytes 589824 | tf_op jit(solution)/shard_map/all_to_all | solution.py:544
  132.9 4.9 %unpack.1 = f32[3,64,128]{2,1,0:T(8,128)} custom-call(f32[576,128]{1,0:T(8,128)} %bitcast.42, s32[64,128]{1,0:T(8,128)} %bitcast.48, s32[64,128]{1,0:T(8,128)} %convert_element_type.38.refs_3_.refs_2_), custom_call_target="tpu_custom_call" | custom-call | tf_op jit(solution)/shard_map/unpack/pallas_call | solution.py:441
  (63 shorter events, 1.0 us)
Async XLA Ops:
  0.6 8.0 %copy-start.6 = (s32[1,1,8192,1]{2,3,1,0:T(1,128)S(1)}, s32[1,1,8192,1]{2,3,1,0:T(1,128)}, u32[]{:S(2)}) copy-start(s32[1,1,8192,1]{2,3,1,0:T(1,128)} %param.12) | copy-start | bytes 98308
  0.6 8.0 %copy-start.8 = (s32[1,1,8192]{2,1,0:T(1,128)S(1)}, s32[1,1,8192]{2,1,0:T(1,128)}, u32[]{:S(2)}) copy-start(s32[1,1,8192]{2,1,0:T(1,128)} %param.13) | copy-start | bytes 98308
  2.4 9.8 %collective-permute-start = (f32[18432]{0:T(1024)S(1)}, f32[18432]{0:T(1024)S(1)}, u32[]{:S(2)}, u32[]{:S(2)}) collective-permute-start(f32[18432]{0:T(1024)S(1)} %pad_maximum_fusion.8), channel_id=1, source_target_pairs={{0,4},{4,8},{8,12},{12,16},{16,20},{20,24},{24,28},{1,5},{5,9},{9,... | collective-permute-start | bytes 221192 | tf_op jit(solution)/shard_map/ppermute | solution.py:454
  7.3 6.2 %collective-permute-start.1 = (f32[18432]{0:T(1024)S(1)}, f32[18432]{0:T(1024)S(1)}, u32[]{:S(2)}, u32[]{:S(2)}) collective-permute-start(f32[18432]{0:T(1024)S(1)} %pad_maximum_fusion.9), channel_id=1, source_target_pairs={{4,0},{8,4},{12,8},{16,12},{20,16},{24,20},{28,24},{5,1},{9,5},{13... | collective-permute-start | bytes 221192 | tf_op jit(solution)/shard_map/ppermute | solution.py:455
  10.4 3.1 %copy-start = (f32[3,128,512]{2,1,0:T(8,128)S(1)}, f32[3,128,512]{2,1,0:T(8,128)}, u32[]{:S(2)}) copy-start(f32[3,128,512]{2,1,0:T(8,128)} %param.14) | copy-start | bytes 2359300
  10.4 3.2 %copy-start.3 = (f32[128,512]{1,0:T(8,128)S(1)}, f32[128,512]{1,0:T(8,128)}, u32[]{:S(2)}) copy-start(f32[128,512]{1,0:T(8,128)} %param.15) | copy-start | bytes 786436
  12.1 1.8 %copy-start.4 = (f32[2,4,16,128]{3,2,1,0:T(8,128)S(1)}, f32[2,4,16,128]{3,2,1,0:T(8,128)}, u32[]{:S(2)}) copy-start(f32[2,4,16,128]{3,2,1,0:T(8,128)} %param.9) | copy-start | bytes 196612
  12.1 1.8 %copy-start.5 = (f32[2,4,16,128]{3,2,1,0:T(8,128)S(1)}, f32[2,4,16,128]{3,2,1,0:T(8,128)}, u32[]{:S(2)}) copy-start(f32[2,4,16,128]{3,2,1,0:T(8,128)} %param.8) | copy-start | bytes 196612
  12.2 1.8 %copy-start.7 = (f32[4,16,128]{2,1,0:T(8,128)S(1)}, f32[4,16,128]{2,1,0:T(8,128)}, u32[]{:S(2)}) copy-start(f32[4,16,128]{2,1,0:T(8,128)} %param.10) | copy-start | bytes 98308
  13.6 3.3 %copy-start.9 = (s32[4,16,9]{1,0,2:T(4,128)S(1)}, s32[4,16,9]{1,0,2:T(4,128)}, u32[]{:S(2)}) copy-start(s32[4,16,9]{1,0,2:T(4,128)} %param.11) | copy-start | bytes 6916
  14.1 4.4 %collective-permute-start.2 = (f32[6016]{0:T(1024)S(1)}, f32[6016]{0:T(1024)S(1)}, u32[]{:S(2)}, u32[]{:S(2)}) collective-permute-start(f32[6016]{0:T(1024)S(1)} %pad_maximum_fusion.14), channel_id=1, source_target_pairs={{0,1},{1,2},{2,3},{4,5},{5,6},{6,7},{8,9},{9,10},{10,11},{12,13},{... | collective-permute-start | bytes 72200 | tf_op jit(solution)/shard_map/ppermute | solution.py:454
  15.6 4.8 %collective-permute-start.3 = (f32[6016]{0:T(1024)S(1)}, f32[6016]{0:T(1024)S(1)}, u32[]{:S(2)}, u32[]{:S(2)}) collective-permute-start(f32[6016]{0:T(1024)S(1)} %pad_maximum_fusion.15), channel_id=1, source_target_pairs={{1,0},{2,1},{3,2},{5,4},{6,5},{7,6},{9,8},{10,9},{11,10},{13,12},{... | collective-permute-start | bytes 72200 | tf_op jit(solution)/shard_map/ppermute | solution.py:455
  47.6 20.5 %all-to-all-start = ((f32[32,24,128]{2,1,0:T(8,128)}), f32[32,24,128]{2,1,0:T(8,128)S(1)}, u32[]{:S(2)}, u32[]{:S(2)}) async-start(f32[32,24,128]{2,1,0:T(8,128)} %pack.1), calls=%async_computation | async-start | bytes 786432 | tf_op jit(solution)/shard_map/all_to_all | solution.py:513
  68.1 3.6 %copy-start.1 = (f32[32,24,128]{2,1,0:T(8,128)}, f32[32,24,128]{2,1,0:T(8,128)S(1)}, u32[]{:S(2)}) copy-start(f32[32,24,128]{2,1,0:T(8,128)S(1)} %all-to-all-done) | copy-start | bytes 1179652
  81.1 11.7 %copy-start.2 = (f32[3,128,512]{2,1,0:T(8,128)S(1)}, f32[3,128,512]{2,1,0:T(8,128)}, u32[]{:S(2)}) copy-start(f32[3,128,512]{2,1,0:T(8,128)} %get-tuple-element.13) | copy-start | bytes 2359300
  82.0 7.6 %collective-permute-start.4 = (f32[6144]{0:T(1024)S(1)}, f32[6144]{0:T(1024)S(1)}, u32[]{:S(2)}, u32[]{:S(2)}) collective-permute-start(f32[6144]{0:T(1024)S(1)} %bitcast.61), channel_id=1, source_target_pairs={{0,4},{4,8},{8,12},{12,16},{16,20},{20,24},{24,28},{1,5},{5,9},{9,... | collective-permute-start | bytes 73736 | tf_op jit(solution)/shard_map/ppermute | solution.py:454
  87.0 5.8 %collective-permute-start.5 = (f32[6144]{0:T(1024)S(1)}, f32[6144]{0:T(1024)S(1)}, u32[]{:S(2)}, u32[]{:S(2)}) collective-permute-start(f32[6144]{0:T(1024)S(1)} %bitcast.62), channel_id=1, source_target_pairs={{4,0},{8,4},{12,8},{16,12},{20,16},{24,20},{28,24},{5,1},{9,5},{13... | collective-permute-start | bytes 73736 | tf_op jit(solution)/shard_map/ppermute | solution.py:455
  93.1 5.1 %collective-permute-start.6 = (f32[1632]{0:T(1024)S(1)}, f32[1632]{0:T(1024)S(1)}, u32[]{:S(2)}, u32[]{:S(2)}) collective-permute-start(f32[1632]{0:T(1024)S(1)} %reshape.224), channel_id=1, source_target_pairs={{0,1},{1,2},{2,3},{4,5},{5,6},{6,7},{8,9},{9,10},{10,11},{12,13},{... | collective-permute-start | bytes 19592 | tf_op jit(solution)/shard_map/ppermute | solution.py:454
  95.0 3.4 %collective-permute-start.7 = (f32[1632]{0:T(1024)S(1)}, f32[1632]{0:T(1024)S(1)}, u32[]{:S(2)}, u32[]{:S(2)}) collective-permute-start(f32[1632]{0:T(1024)S(1)} %reshape.226), channel_id=1, source_target_pairs={{1,0},{2,1},{3,2},{5,4},{6,5},{7,6},{9,8},{10,9},{11,10},{13,12},{... | collective-permute-start | bytes 19592 | tf_op jit(solution)/shard_map/ppermute | solution.py:455

commit v3 on v2

--- a/solution.py
+++ b/solution.py
@@ -66,14 +66,23 @@
     return jnp.broadcast_to(row, (LANES, row.shape[1])).T
 
 
-def sph_kernel(present_ref, pad_ref, density_ref, source_ref, uv_ref, carry_ref, col_ref, acc_ref, sums_ref):
+def thirds(values):
+    first = values.astype(jnp.bfloat16).astype(jnp.float32)
+    second = (values - first).astype(jnp.bfloat16).astype(jnp.float32)
+    return first, second, values - first - second
+
+
+AHEAD = 4
+
+
+def sph_kernel(
+    present_ref, pad_ref, density_ref, source_ref, carry_ref, right_ref, shift_ref, sums_ref, *scratch
+):
     _, rows2, cols2, size = pad_ref.shape
     rows, cols = rows2 - 2, cols2 - 2
     tiles = rows * cols
+    left_refs, exponent_refs, acc_refs = scratch[:AHEAD], scratch[AHEAD : 2 * AHEAD], scratch[2 * AHEAD :]
     x, y, vx, vy, m = [pad_ref[k] for k in range(5)]
-    for d in range(3):
-        uv_ref[d] = (2.0 * LOG2E) * (x + (d - 1.0))
-        uv_ref[3 + d] = (2.0 * LOG2E) * (y + (d - 1.0))
     gx = [jnp.exp2(-LOG2E * (x + (d - 1.0)) * (x + (d - 1.0))) for d in range(3)]
     gy = [jnp.exp2(-LOG2E * (y + (d - 1.0)) * (y + (d - 1.0))) for d in range(3)]
     for di in range(3):
@@ -82,46 +91,74 @@
             carry_ref[3 * (3 * di + dj)] = g
             carry_ref[3 * (3 * di + dj) + 1] = g * vx
             carry_ref[3 * (3 * di + dj) + 2] = g * vy
+    right_ref[...] = jnp.zeros_like(right_ref)
+    for c, place in enumerate((x, y)):
+        for n, part in enumerate(thirds((2.0 * LOG2E) * place)):
+            for i in range(rows2):
+                right_ref[i, :, 3 * c + n, :] = part[i]
+    unit = thirds(jnp.full((1, size), 2.0 * LOG2E, jnp.float32))
+    none = jnp.zeros((2, size), jnp.float32)
+    for w in range(9):
+        shift_ref[w] = jnp.concatenate([part * (d - 1.0) for d in (w // 3, w % 3) for part in unit] + [none], axis=0)
+    sublane = lax.broadcasted_iota(jnp.int32, (8, size), 0)
 
     def prepare(t, slot):
+        own = [thirds(pad_ref[k, t // cols + 1, pl.ds(t % cols + 1, 1), :]) for k in range(2)]
+        lefts = []
+        for n in range(3):
+            lefts.append(
+                jnp.where(sublane < 3 - n, own[0][n], jnp.where((sublane >= 3) & (sublane < 6 - n), own[1][n], 0.0))
+            )
+        flagged = jnp.where(sublane == 6, 1.0, lefts[0])
+        left_refs[slot][...] = jnp.concatenate(lefts + [flagged] + lefts[1:], axis=0).T.astype(jnp.bfloat16)
+
+    def expand(t, slot):
         i, j = t // cols, t % cols
-        for k in range(2):
-            col_ref[slot, k] = columns_of(pad_ref[k, i + 1, pl.ds(j + 1, 1), :])
+        right = []
+        absent = jnp.where(sublane == 6, -1024.0, 0.0)
+        for w in range(9):
+            near = right_ref[i + w // 3, j + w % 3]
+            shift = shift_ref[w] + absent * (1.0 - present_ref[t * 9 + w])
+            right.append(jnp.concatenate([near] * 3 + [shift] * 3, axis=0).astype(jnp.bfloat16))
+        exponent_refs[slot][...] = jnp.dot(
+            left_refs[slot][...], jnp.concatenate(right, axis=1), preferred_element_type=jnp.float32
+        )
 
     def finish(t, slot):
         for k in range(3):
-            sums_ref[k, pl.ds(t, 1), :] = jnp.sum(acc_ref[slot, k].T, axis=0, keepdims=True)
+            sums_ref[k, pl.ds(t, 1), :] = jnp.sum(acc_refs[slot][k].T, axis=0, keepdims=True)
 
     def compute(t, slot):
         i, j = t // cols, t % cols
         half = size // 2
         for h in range(2):
-            xa = col_ref[slot, 0, h * half : (h + 1) * half, :]
-            ya = col_ref[slot, 1, h * half : (h + 1) * half, :]
             acc = [jnp.zeros((half, size), jnp.float32) for _ in range(3)]
             for w in range(9):
-                di, dj = w // 3, w % 3
-                there = present_ref[t * 9 + w]
-                u = uv_ref[di, i + di, pl.ds(j + dj, 1), :]
-                v = uv_ref[3 + dj, i + di, pl.ds(j + dj, 1), :]
-                weight = jnp.exp2(xa * u + ya * v)
+                weight = jnp.exp2(exponent_refs[slot][h * half : (h + 1) * half, w * size : (w + 1) * size])
                 for k in range(3):
-                    acc[k] = acc[k] + weight * (carry_ref[3 * w + k, i + di, pl.ds(j + dj, 1), :] * there)
+                    acc[k] = acc[k] + weight * carry_ref[3 * w + k, i + w // 3, pl.ds(j + w % 3, 1), :]
             for k in range(3):
-                acc_ref[slot, k, h * half : (h + 1) * half, :] = acc[k]
-
-    prepare(0, 0)
+                acc_refs[slot][k, h * half : (h + 1) * half, :] = acc[k]
+
+    last = tiles - 1
+    unroll = math.gcd(4 * AHEAD, tiles)
+    for t in range(3):
+        prepare(t, t)
+    for t in range(2):
+        expand(t, t)
 
     def step(p, _):
-        for slot in range(2):
-            t = 2 * p + slot
-            prepare(jnp.minimum(t + 1, tiles - 1), 1 - slot)
-            finish(jnp.maximum(t - 1, 0), 1 - slot)
-            compute(t, slot)
+        for m in range(unroll):
+            t = unroll * p + m
+            n = m % AHEAD
+            prepare(jnp.minimum(t + 3, last), (n + 3) % AHEAD)
+            expand(jnp.minimum(t + 2, last), (n + 2) % AHEAD)
+            finish(jnp.maximum(t - 1, 0), (n - 1) % AHEAD)
+            compute(t, n)
         return 0
 
-    lax.fori_loop(0, tiles // 2, step, 0)
-    finish(tiles - 1, (tiles - 1) % 2)
+    lax.fori_loop(0, tiles // unroll, step, 0)
+    finish(last, last % AHEAD)
 
     for i in range(rows):
         own = pad_ref[:, i + 1, 1 : cols + 1, :]
@@ -149,12 +186,14 @@
         in_specs=[smem(), vmem()],
         out_specs=(vmem(), vmem()),
         scratch_shapes=[
-            pltpu.VMEM((6, rows2, cols2, size), jnp.float32),
             pltpu.VMEM((27, rows2, cols2, size), jnp.float32),
-            pltpu.VMEM((2, 2, size, size), jnp.float32),
-            pltpu.VMEM((2, 3, size, size), jnp.float32),
+            pltpu.VMEM((rows2, cols2, 8, size), jnp.float32),
+            pltpu.VMEM((9, 8, size), jnp.float32),
             pltpu.VMEM((3, rows * cols, size), jnp.float32),
-        ],
+        ]
+        + [pltpu.VMEM((size, 48), jnp.bfloat16)] * AHEAD
+        + [pltpu.VMEM((size, 9 * size), jnp.float32)] * AHEAD
+        + [pltpu.VMEM((3, size, size), jnp.float32)] * AHEAD,
         compiler_params=pltpu.CompilerParams(vmem_limit_bytes=VMEM_LIMIT),
         name="sph",
     )(present, padded)
@@ -222,9 +261,10 @@
 
 
 GROUP = 16
-
-
-def list_blocks(start_ref, amount_ref, block_ref, bound_ref, *, senders, bins, blocks):
+UNROLL = 3
+
+
+def list_blocks(plan_ref, block_ref, *, senders, bins, blocks):
     total = 0
     together = math.gcd(8, senders)
     for q in range(bins):
@@ -232,23 +272,23 @@
         def some(g, total):
             for n in range(together):
                 s = g * together + n
-                first = 4 * blocks * s + start_ref[s * bins + q]
+                first = 4 * blocks * s + plan_ref[s * bins + q]
                 for b in range(blocks):
                     block_ref[total + b] = first + b
-                total = total + amount_ref[s * bins + q]
+                total = total + plan_ref[(senders + s) * bins + q]
             return total
 
         total = lax.fori_loop(0, senders // together, some, total)
         for b in range(GROUP):
             block_ref[total + b] = -1
         total = (total + GROUP - 1) // GROUP * GROUP
-        bound_ref[q] = total // GROUP
-    for b in range(3 * GROUP):
+        block_ref[bounds_at(senders, bins, blocks) + q] = total // GROUP
+    for b in range(UNROLL * GROUP):
         block_ref[total + b] = -1
 
 
-def list_sizes(senders, bins, blocks):
-    return senders * (blocks + bins) + (bins + 4) * GROUP, bins
+def bounds_at(senders, bins, blocks):
+    return senders * (blocks + bins) + (bins + UNROLL + 1) * GROUP
 
 
 def bin_of(group, bound_ref, bins):
@@ -259,12 +299,12 @@
 
 
 def by_group(bound_ref, bins, work):
-    def pair(p, _):
-        for n in range(2):
-            work(2 * p + n)
+    def some(p, _):
+        for n in range(UNROLL):
+            work(UNROLL * p + n)
         return 0
 
-    lax.fori_loop(0, (bound_ref[bins - 1] + 1) // 2, pair, 0)
+    lax.fori_loop(0, (bound_ref[bins - 1] + UNROLL - 1) // UNROLL, some, 0)
 
 
 def block_cells(in_ref, row, base, cells_cross):
@@ -273,10 +313,11 @@
     return there, row_of - jnp.where(row < 0, 1 << 20, base).astype(jnp.float32), col_of
 
 
-def deposit_kernel(start_ref, amount_ref, in_ref, out_ref, block_ref, bound_ref, *, senders, bins, blocks):
+def deposit_kernel(plan_ref, in_ref, out_ref, first_ref, second_ref, block_ref, *, senders, bins, blocks):
     _, cells_along, cells_cross = out_ref.shape
     height = cells_along // bins
-    list_blocks(start_ref, amount_ref, block_ref, bound_ref, senders=senders, bins=bins, blocks=blocks)
+    list_blocks(plan_ref, block_ref, senders=senders, bins=bins, blocks=blocks)
+    bound_ref = block_ref.at[pl.ds(bounds_at(senders, bins, blocks), bins)]
     out_ref[...] = jnp.zeros_like(out_ref)
 
     def work(group):
@@ -300,67 +341,79 @@
             out_ref[k, pl.ds(pl.multiple_of(base, height), height), :] += part
 
     by_group(bound_ref, bins, work)
-
-
-def deposit(incoming, starts, amounts, bins, cells_along, cells_cross):
+    margin = first_ref.shape[1]
+    even = plan_ref[2 * senders * bins] > 0
+    top, bottom = out_ref[:, :margin, :], out_ref[:, cells_along - margin :, :]
+    first_ref[...] = jnp.where(even, bottom, top)
+    second_ref[...] = jnp.where(even, top, bottom)
+
+
+def deposit(incoming, plan, bins, margin, cells_along, cells_cross):
     senders = incoming.shape[0]
     blocks = incoming.shape[1] // 4
-    size, bounds = list_sizes(senders, bins, blocks)
     return pl.pallas_call(
         lambda *refs: deposit_kernel(*refs, senders=senders, bins=bins, blocks=blocks),
         out_shape=(
             jax.ShapeDtypeStruct((3, cells_along, cells_cross), jnp.float32),
-            jax.ShapeDtypeStruct((size,), jnp.int32),
-            jax.ShapeDtypeStruct((bounds,), jnp.int32),
+            jax.ShapeDtypeStruct((3, margin, cells_cross), jnp.float32),
+            jax.ShapeDtypeStruct((3, margin, cells_cross), jnp.float32),
+            jax.ShapeDtypeStruct((bounds_at(senders, bins, blocks) + bins,), jnp.int32),
         ),
-        in_specs=[smem(), smem(), vmem()],
-        out_specs=(vmem(), smem(), smem()),
+        in_specs=[smem(), vmem()],
+        out_specs=(vmem(), vmem(), vmem(), smem()),
         compiler_params=pltpu.CompilerParams(vmem_limit_bytes=VMEM_LIMIT),
         name="deposit",
-    )(starts, amounts, incoming.reshape(-1, LANES))
-
-
-def substeps(edge_ref, water_ref, source_ref, state_ref, margin):
+    )(plan, incoming.reshape(-1, LANES))
+
+
+def substeps(edge_ref, water_ref, source_ref, state_ref, margin, *fields):
     _, cells_along, cells_cross = state_ref.shape
-    _, height, width = water_ref.shape
-    rows = lax.broadcasted_iota(jnp.int32, (height, width), 0)
-    cols = lax.broadcasted_iota(jnp.int32, (height, width), 1)
-    inside = (rows >= edge_ref[0]) & (rows < edge_ref[1]) & (cols >= edge_ref[2]) & (cols < edge_ref[3])
-
-    def along(field):
-        return pltpu.roll(field, height - 1, 0), pltpu.roll(field, 1, 0)
-
-    def cross(field):
-        return pltpu.roll(field, width - 1, 1), pltpu.roll(field, 1, 1)
-
-    depth = water_ref[3]
-    elevation, speed_x, speed_y = water_ref[0], water_ref[1], water_ref[2]
-    for _ in range(SUBSTEPS):
-        east, west = along(elevation)
-        north, south = cross(elevation)
-        flux_east, flux_west = along(depth * speed_x)
-        flux_north, flux_south = cross(depth * speed_y)
-        around = [sum(along(f) + cross(f)) for f in (speed_x, speed_y)]
-        flow = flux_east - flux_west + flux_north - flux_south
-        following = (
-            0.25 * (east + west + north + south) - 0.5 * courant * flow,
-            0.25 * around[0] - 0.5 * courant * (east - west),
-            0.25 * around[1] - 0.5 * courant * (north - south),
-        )
-        elevation, speed_x, speed_y = [
-            jnp.where(inside, value + source_ref[k], 0.0) for k, value in enumerate(following)
-        ]
-    for k, field in enumerate((elevation, speed_x, speed_y)):
-        field = pltpu.roll(pltpu.roll(field, height - margin, 0), width - margin, 1)
-        state_ref[k] = field[:cells_along, :cells_cross]
+    _, height, width = source_ref.shape
+    groups = height // 8
+    slope = 0.5 * courant
+    rows = lax.broadcasted_iota(jnp.int32, (8, width), 0)
+    cols = lax.broadcasted_iota(jnp.int32, (8, width), 1)
+    inside_cols = (cols >= edge_ref[2]) & (cols < edge_ref[3])
+    nothing = [jnp.zeros((8, width), jnp.float32)] * 3
+
+    def terms(old, g):
+        at = slice(8 * g, 8 * g + 8)
+        h, u, v = [old[k, at, :] for k in range(3)]
+        depth = slope * water_ref[3, at, :]
+        flux_x, flux_y, height_x = depth * u, depth * v, slope * h
+        h, u, v = 0.25 * h, 0.25 * u, 0.25 * v
+        east = [pltpu.roll(term, 7, 0) for term in (h - flux_x, u - height_x, v)]
+        west = [pltpu.roll(term, 1, 0) for term in (h + flux_x, u + height_x, v)]
+        north = [pltpu.roll(term, width - 1, 1) for term in (h - flux_y, u, v - height_x)]
+        south = [pltpu.roll(term, 1, 1) for term in (h + flux_y, u, v + height_x)]
+        return east, west, [a + b for a, b in zip(north, south)]
+
+    old = water_ref
+    for n in range(SUBSTEPS):
+        new = fields[n % 2]
+        before, (east, west, across) = nothing, terms(old, 0)
+        for g in range(groups):
+            after = terms(old, g + 1) if g + 1 < groups else (nothing, nothing, nothing)
+            inside = inside_cols & (rows >= edge_ref[0] - 8 * g) & (rows < edge_ref[1] - 8 * g)
+            for k in range(3):
+                value = jnp.where(rows == 7, after[0][k], east[k]) + jnp.where(rows == 0, before[k], west[k])
+                value = value + across[k] + source_ref[k, 8 * g : 8 * g + 8, :]
+                new[k, 8 * g : 8 * g + 8, :] = jnp.where(inside, value, 0.0)
+            before, (east, west, across) = west, after
+        old = new
+    for k in range(3):
+        for first in range(0, cells_along, 8):
+            block = old[k, margin + first : margin + first + 8, :]
+            state_ref[k, first : first + 8, :] = pltpu.roll(block, width - margin, 1)[:, :cells_cross]
 
 
 def lookup_kernel(
-    block_ref, bound_ref, edge_ref, in_ref, water_ref, source_ref, out_ref, state_ref, left_ref, *, bins, blocks, margin
+    block_ref, edge_ref, in_ref, water_ref, source_ref, out_ref, state_ref, left_ref, *fields, bins, blocks, margin
 ):
     _, cells_along, cells_cross = state_ref.shape
     height = cells_along // bins
-    substeps(edge_ref, water_ref, source_ref, state_ref, margin)
+    bound_ref = block_ref.at[pl.ds(bounds_at(in_ref.shape[0] // (4 * blocks), bins, blocks), bins)]
+    substeps(edge_ref, water_ref, source_ref, state_ref, margin, *fields)
     for k in range(3):
         for h, value in enumerate(split(state_ref[k])):
             q = 2 * k + h
@@ -390,7 +443,7 @@
     by_group(bound_ref, bins, work)
 
 
-def lookup(incoming, block_list, bounds, edges, water, source, bins, margin, cells_along, cells_cross):
+def lookup(incoming, block_list, edges, water, source, bins, margin, cells_along, cells_cross):
     senders, rows, _ = incoming.shape
     return pl.pallas_call(
         lambda *refs: lookup_kernel(*refs, bins=bins, blocks=rows // 4, margin=margin),
@@ -398,12 +451,13 @@
             jax.ShapeDtypeStruct((senders * rows // 4 * 3, LANES), jnp.float32),
             jax.ShapeDtypeStruct((3, cells_along, cells_cross), jnp.float32),
         ),
-        in_specs=[smem()] * 3 + [vmem()] * 3,
+        in_specs=[smem()] * 2 + [vmem()] * 3,
         out_specs=(vmem(), vmem()),
-        scratch_shapes=[pltpu.VMEM((bins, 6 * cells_along // bins, cells_cross), jnp.bfloat16)],
+        scratch_shapes=[pltpu.VMEM((bins, 6 * cells_along // bins, cells_cross), jnp.bfloat16)]
+        + [pltpu.VMEM((3,) + water.shape[1:], jnp.float32)] * 2,
         compiler_params=pltpu.CompilerParams(vmem_limit_bytes=VMEM_LIMIT),
         name="lookup",
-    )(block_list, bounds, edges, incoming.reshape(-1, LANES), water, source)
+    )(block_list, edges, incoming.reshape(-1, LANES), water, source)
 
 
 def unpack_kernel(in_ref, dest_ref, rank_ref, out_ref, left_ref, *, capacity, group):
@@ -449,11 +503,23 @@
     )(returned, dest, rank)
 
 
-def swap(axis, to_next, to_previous):
+def is_even(axis):
+    return lax.axis_index(axis) % 2 == 0
+
+
+def swap(axis, first, second):
     count = lax.axis_size(axis)
-    before = lax.ppermute(to_next, axis, [(i, i + 1) for i in range(count - 1)])
-    after = lax.ppermute(to_previous, axis, [(i + 1, i) for i in range(count - 1)])
-    return before, after
+    arrived = []
+    for offset, payload in enumerate((first, second)):
+        pairs = [(i, i + 1) for i in range(offset, count - 1, 2)]
+        arrived.append(lax.ppermute(payload, axis, pairs + [(j, i) for i, j in pairs]))
+    even = is_even(axis)
+    return jnp.where(even, arrived[1], arrived[0]), jnp.where(even, arrived[0], arrived[1])
+
+
+def in_order(axis, to_next, to_previous):
+    even = is_even(axis)
+    return jnp.where(even, to_next, to_previous), jnp.where(even, to_previous, to_next)
 
 
 def padded_together(fields):
@@ -465,7 +531,7 @@
             heads.append(lax.slice_in_dim(array, 0, width, axis=dim))
             tails.append(lax.slice_in_dim(array, array.shape[dim] - width, array.shape[dim], axis=dim))
         flat = lambda parts: jnp.concatenate([part.reshape(-1) for part in parts])
-        before, after = swap(axis, flat(tails), flat(heads))
+        before, after = swap(axis, *in_order(axis, flat(tails), flat(heads)))
         start, grown = 0, []
         for array, head, (_, dims, _) in zip(arrays, heads, fields):
             rims = [rim[start : start + head.size].reshape(head.shape) for rim in (before, after)]
@@ -512,17 +578,23 @@
     outgoing = pack(sources, cell, destination, rank, devices, capacity)
     incoming = lax.all_to_all(outgoing, ("along", "cross"), split_axis=0, concat_axis=0, tiled=True)
     blocks = capacity // LANES
-    filled = incoming[:, blocks : 2 * blocks] != 0.0
-    bin_in = jnp.floor(incoming[:, :blocks] * (bins / (cells_along * cells_cross)))
-    counts = jnp.stack([jnp.sum((filled & (bin_in == q)).astype(jnp.int32), axis=(1, 2)) for q in range(bins)], axis=1)
-    ends = jnp.cumsum(counts, axis=1)
-    starts = (ends - counts) // LANES
-    amounts = jnp.where(counts > 0, (ends + LANES - 1) // LANES - starts, 0)
-    grid_source, block_list, bounds = deposit(
-        incoming, starts.reshape(-1), amounts.reshape(-1), bins, cells_along, cells_cross
+    to_bin = bins / (cells_along * cells_cross)
+    lowest = jnp.floor(incoming[:, :blocks, 0] * to_bin)[..., None]
+    highest = jnp.floor(jnp.max(incoming[:, :blocks], axis=2) * to_bin)[..., None]
+    filled = (incoming[:, blocks : 2 * blocks, 0] != 0.0)[..., None]
+    each = jnp.arange(bins, dtype=jnp.float32)
+    plan = jnp.stack(
+        [
+            jnp.sum((filled & (highest < each)).astype(jnp.int32), axis=1),
+            jnp.sum((filled & (lowest <= each) & (highest >= each)).astype(jnp.int32), axis=1),
+        ]
     )
-    (wide_source,) = padded_together([(grid_source, (1, 2), margin)])
-
+    plan = jnp.concatenate([plan.reshape(-1), is_even("along").astype(jnp.int32)[None]])
+    grid_source, first, second, block_list = deposit(incoming, plan, bins, margin, cells_along, cells_cross)
+    before, after = swap("along", first, second)
+    tall = jnp.concatenate([before, grid_source, after], axis=1)
+    before, after = swap("cross", *in_order("cross", tall[:, :, cells_cross - margin :], tall[:, :, :margin]))
+    wide_source = jnp.concatenate([before, tall, after], axis=2)
     edges = []
     for axis, length in (("along", cells_along), ("cross", cells_cross)):
         place = lax.axis_index(axis)
@@ -532,7 +604,6 @@
     looked, water_state = lookup(
         incoming,
         block_list,
-        bounds,
         jnp.stack(edges).astype(jnp.int32),
         jnp.pad(wide_water, to_lanes),
         jnp.pad(wide_source, to_lanes),

time: 140 us -> 122 us (0.87); the launches traced: 138 us -> 125 us
  starting transfers between devices: 25.5 us -> 18.9 us
  blocking collectives: 19.3 us -> 25.2 us
  waiting for transfers between devices: 19.7 us -> 14.1 us
  Pallas kernels: 54.2 us -> 50.3 us
  local copies, waits for them, and re-layouts: 4.43 us -> 2.9 us
    all_to_all x1, blocking collectives: 19.3 us -> 25.2 us  [shards(): lax.all_to_all(looked.reshape(devices, 3 * capacity), ('along', 'cross'),...]
    ppermute x8, waiting for transfers between devices: 6.48 us -> 0.87 us  [swap(): lax.ppermute(payload, axis, pairs + [(j, i) for i, j in pairs])]
    pallas_call x1, Pallas kernels: 20.3 us -> 15.2 us  [sph(): pl.pallas_call(sph_kernel, out_shape=(jax.ShapeDtypeStruct((rows, cols, s...]
    ppermute x8, starting transfers between devices: 18.3 us -> 14.1 us  [swap(): lax.ppermute(payload, axis, pairs + [(j, i) for i, j in pairs])]
    all_to_all x1, starting transfers between devices: 7.22 us -> 4.74 us  [shards(): lax.all_to_all(outgoing, ('along', 'cross'), split_axis=0, concat_axis=0,...]
    reduce_sum x1, other arithmetic: 2.36 us -> 0.03 us  [shards(): jnp.sum((filled & (highest < each)).astype(jnp.int32), axis=1)]
    concatenate x4 -> x2, other arithmetic: 0.03 us -> 1.96 us  [the longest x1 1.4 us: shards(): wide_source = jnp.concatenate([before, tall, after], axis=2)]
    concatenate x3 -> x2, other arithmetic: 3.89 us -> 2.49 us  [padded_together(): grown.append(jnp.concatenate([rims[0], array, rims[1]], axis=dims[step]))]
  transfers between devices with their start and end apart: 9 -> 9, of which waited for: 4 -> 2; matrix products, arithmetic and copies ran while one was open for 6% -> 6% of each run, Pallas kernels for 0% -> 0%
where the time goes in v3:
time: 122 us; the launch traced here: 125 us
  Pallas kernels  50.3 us (41%)
  blocking collectives  25.2 us (21%)
  starting transfers between devices  18.9 us (15%)
  waiting for transfers between devices  14.1 us (12%)
  other arithmetic  10.7 us (9%)
  local copies, waits for them, and re-layouts  2.9 us (2%)
  matrix products  1.69 us (1%)
    all_to_all x1, blocking collectives, shards(): lax.all_to_all(looked.reshape(devices, 3 * capacity), ('along', 'cross'),...  25.2 us
    pallas_call x1, Pallas kernels, sph(): pl.pallas_call(sph_kernel, out_shape=(jax.ShapeDtypeStruct((rows, cols, s...  15.2 us
    ppermute x8, starting transfers between devices, swap(): lax.ppermute(payload, axis, pairs + [(j, i) for i, j in pairs])  14.1 us
    pallas_call x1, Pallas kernels, lookup(): pl.pallas_call(lambda *refs: lookup_kernel(*refs, bins=bins, blocks=rows...  13.7 us
    all_to_all x1, waiting for transfers between devices, shards(): lax.all_to_all(outgoing, ('along', 'cross'), split_axis=0, concat_axis=0,...  13.2 us
    pallas_call x1, Pallas kernels, deposit(): pl.pallas_call(lambda *refs: deposit_kernel(*refs, senders=senders, bins=...  10.4 us
    pallas_call x1, Pallas kernels, pack(): pl.pallas_call(lambda *refs: pack_kernel(*refs, group=group), out_shape=j...  6.05 us
    pallas_call x1, Pallas kernels, unpack(): pl.pallas_call(lambda *refs: unpack_kernel(*refs, capacity=capacity, grou...  4.94 us
  transfers between devices with their start and end apart: 9, of which 2 were waited for; matrix products, arithmetic and copies ran while one was open for 6% of the time, Pallas kernels for 0%

profile of v3, /device:TPU:0, one launch (start us, length us, event | category | flops | bytes accessed | tf_op | source)
XLA Modules:
  0.0 124.8 jit_solution(15608003521119108119)
XLA Ops:
  0.7 0.9 maximum_bitcast_fusion
  1.6 0.8 pad_maximum_fusion.12
  2.4 0.7 collective-permute-start
  3.1 5.8 %collective-permute-start.1 = (f32[18432]{0:T(1024)S(1)}, f32[18432]{0:T(1024)S(1)}, u32[]{:S(2)}, u32[]{:S(2)}) collective-permute-start(f32[18432]{0:T(1024)S(1)} %get-tuple-element.39), channel_id=1, source_target_pairs={{0,4},{8,12},{16,20},{24,28},{4,0},{12,8},{20,16},{28,24},{1,5},{9... | collective-permute-start | bytes 221192 | tf_op jit(solution)/shard_map/ppermute | solution.py:515
  8.9 1.3 %convert_reduce_fusion = (f32[128]{0:T(128)S(1)}, f32[64,128]{1,0:T(8,128)S(1)}) fusion(s32[64,128]{1,0:T(8,128)S(1)} %fusion.23), kind=kLoop, calls=%fused_computation.1 | loop fusion | flops 5234560 | bytes 66048 | tf_op jit(solution)/shard_map/reduce_sum | solution.py:550
  10.2 0.1 reshape.188
  10.3 0.2 reduce_window_sum.25
  10.5 0.1 reduce_window_sum.26
  10.6 0.1 reduce_window_sum.24
  10.7 1.7 %fusion = f32[64,128]{1,0:T(8,128)S(1)} fusion(f32[64,128]{1,0:T(8,128)S(1)} %subtract_add_fusion, s32[64,128]{1,0:T(8,128)S(1)} %fusion.23), kind=kOutput, calls=%fused_computation.3 | convolution fusion | flops 275783680 | bytes 98304 | tf_op jit(solution)/shard_map/ij,bjd->bid/dot_general | solution.py:548
  12.7 0.2 pad_maximum_fusion.4
  12.8 0.2 reshape.181
  13.0 0.2 reshape.183
  13.2 0.2 copy-done.4
  13.4 0.1 maximum_reduce_fusion
  13.6 0.7 collective-permute-start.2
  14.2 2.9 %collective-permute-start.3 = (f32[6016]{0:T(1024)S(1)}, f32[6016]{0:T(1024)S(1)}, u32[]{:S(2)}, u32[]{:S(2)}) collective-permute-start(f32[6016]{0:T(1024)S(1)} %get-tuple-element.45), channel_id=1, source_target_pairs={{0,1},{2,3},{1,0},{3,2},{4,5},{6,7},{5,4},{7,6},{8,9},{10,11},{9,8... | collective-permute-start | bytes 72200 | tf_op jit(solution)/shard_map/ppermute | solution.py:515
  17.2 0.1 fusion.16
  17.3 0.1 copy.36
  17.4 0.7 reshape.195.present_ref
  18.1 0.6 convert_element_type.33.refs_3_.refs_2_
  18.8 0.8 pad_maximum_fusion.pad_ref
  19.6 15.2 %sph.1 = (f32[4,16,128]{2,1,0:T(8,128)}, f32[3,64,128]{2,1,0:T(8,128)}) custom-call(f32[576]{0:T(1024)} %reshape.195.present_ref, f32[5,6,18,128]{3,2,1,0:T(8,128)} %pad_maximum_fusion.pad_ref), custom_call_target="tpu_custom_call" | custom-call | tf_op jit(solution)/shard_map/sph/pallas_call | solution.py:180
  34.8 6.0 %pack.1 = f32[32,24,128]{2,1,0:T(8,128)} custom-call(f32[3,64,128]{2,1,0:T(8,128)} %get-tuple-element.11.refs_0_, s32[64,128]{1,0:T(8,128)} %bitcast.51, s32[64,128]{1,0:T(8,128)} %bitcast.42, s32[64,128]{1,0:T(8,128)} %convert_element_type.33.refs_3_.refs_2_), custom_call_target="tpu_custom_call" | custom-call | tf_op jit(solution)/shard_map/pack/pallas_call | solution.py:247
  40.9 4.7 %all-to-all-start = ((f32[32,24,128]{2,1,0:T(8,128)}), f32[32,24,128]{2,1,0:T(8,128)S(1)}, u32[]{:S(2)}, u32[]{:S(2)}) async-start(f32[32,24,128]{2,1,0:T(8,128)} %pack.1), calls=%async_computation | async-start | bytes 786432 | tf_op jit(solution)/shard_map/all_to_all | solution.py:579
  45.6 13.2 %all-to-all-done = f32[32,24,128]{2,1,0:T(8,128)S(1)} async-done(((f32[32,24,128]{2,1,0:T(8,128)}), f32[32,24,128]{2,1,0:T(8,128)S(1)}, u32[]{:S(2)}, u32[]{:S(2)}) %all-to-all-start) | async-done | bytes 393248 | tf_op jit(solution)/shard_map/all_to_all | solution.py:579
  58.9 0.1 copy.41
  59.0 0.1 copy.38
  59.2 0.1 slice_reduce_fusion
  59.3 0.1 copy.39
  59.4 0.1 copy.42
  59.5 0.1 reshape.189
  59.6 0.6 pad_add_fusion.1.refs_0_
  60.2 10.4 %deposit.1 = (f32[3,128,512]{2,1,0:T(8,128)}, f32[3,4,512]{2,1,0:T(4,128)}, f32[3,4,512]{2,1,0:T(4,128)}, s32[452]{0:T(512)}) custom-call(s32[257]{0:T(512)} %pad_add_fusion.1.refs_0_, f32[768,128]{1,0:T(8,128)} %bitcast.32), custom_call_target="tpu_custom_call" | custom-call | tf_op jit(solution)/shard_map/deposit/pallas_call | solution.py:354
  70.6 0.7 collective-permute-start.4
  71.3 2.2 %collective-permute-start.5 = (f32[3,4,512]{2,1,0:T(4,128)}, f32[3,4,512]{2,1,0:T(4,128)S(1)}, u32[]{:S(2)}, u32[]{:S(2)}) collective-permute-start(f32[3,4,512]{2,1,0:T(4,128)} %get-tuple-element.14), channel_id=1, source_target_pairs={{0,4},{8,12},{16,20},{24,28},{4,0},{12,8},{20,16},{28,24},{1,5},{9... | collective-permute-start | bytes 73736 | tf_op jit(solution)/shard_map/ppermute | solution.py:515
  73.5 0.6 pad_add_fusion.2.refs_1_
  74.1 0.3 reshape.191
  74.4 0.3 reshape.192
  74.7 0.8 collective-permute-done.5
  75.5 1.2 broadcast_select_fusion.3
  76.7 0.2 collective-permute-start.7
  76.9 1.0 collective-permute-start.6
  77.9 1.7 %select_maximum_fusion.refs_3_ = f32[4,136,640]{2,1,0:T(8,128)} fusion(f32[4,136,4]{2,1,0:T(8,128)S(1)} %reshape.192, f32[4,136,4]{2,1,0:T(8,128)S(1)} %reshape.191, f32[4,4,512]{2,1,0:T(4,128)S(1)} %slice.115, f32[4,4,512]{2,1,0:T(4,128)S(1)} %slice.113, f32[1,128,512]{2,1,0:T(8,128)S(1)} %bitcast.36, f32[3,128,512]{2,1,0:T(8,128)S(1)} %copy-done), kind=kLoop, calls=%fused_computation.8 | loop fusion | flops 4177920 | bytes 2524160 | tf_op jit(solution)/shard_map/concatenate | solution.py:539
  79.7 1.4 %select_maximum_fusion.2.refs_4_ = f32[3,136,640]{2,1,0:T(8,128)} fusion(f32[3,136,4]{2,1,0:T(8,128)S(1)} %get-tuple-element.33, f32[3,136,4]{2,1,0:T(8,128)S(1)} %get-tuple-element.32, f32[3,4,512]{2,1,0:T(4,128)S(1)} %get-tuple-element.41, f32[3,128,512]{2,1,0:T(8,128)S(1)} %copy-done.2, f32[3,4,512]{2,1,0:T(4,128)S(1)} %get-tuple-element.40), kind=kLoop, calls=%fused_computation.18 | loop fusion | flops 2611200 | bytes 1893120 | tf_op jit(solution)/shard_map/concatenate | solution.py:597
  81.1 13.7 %lookup.1 = (f32[576,128]{1,0:T(8,128)}, f32[3,128,512]{2,1,0:T(8,128)}) custom-call(s32[452]{0:T(512)} %get-tuple-element.12.refs_0_, s32[4]{0:T(128)} %pad_add_fusion.2.refs_1_, f32[768,128]{1,0:T(8,128)} %bitcast.33, f32[4,136,640]{2,1,0:T(8,128)} %select_maximum_fusion.refs_3_, f32[3,136,640]{2,1,0:T(8,128)} %select_maximum_fusion.2.refs_4_), custom_call_target="tpu_custom_call" | custom-call | tf_op jit(solution)/shard_map/lookup/pallas_call | solution.py:448
  94.7 25.2 %all_to_all.14 = f32[32,1,2304]{2,1,0:T(1,128)} all-to-all(f32[32,1,2304]{2,1,0:T(1,128)} %bitcast.48), channel_id=1, replica_groups=mesh['along'=8,'cross'=4] {'along','cross'}, dimensions={0} | all-to-all | bytes 589824 | tf_op jit(solution)/shard_map/all_to_all | solution.py:615
  119.9 4.9 %unpack.1 = f32[3,64,128]{2,1,0:T(8,128)} custom-call(f32[576,128]{1,0:T(8,128)} %bitcast.37, s32[64,128]{1,0:T(8,128)} %bitcast.43, s32[64,128]{1,0:T(8,128)} %convert_element_type.33.refs_3_.refs_2_), custom_call_target="tpu_custom_call" | custom-call | tf_op jit(solution)/shard_map/unpack/pallas_call | solution.py:495
  (63 shorter events, 0.5 us)
Async XLA Ops:
  0.6 8.3 %copy-start.6 = (s32[1,1,8192,1]{2,3,1,0:T(1,128)S(1)}, s32[1,1,8192,1]{2,3,1,0:T(1,128)}, u32[]{:S(2)}) copy-start(s32[1,1,8192,1]{2,3,1,0:T(1,128)} %param.12) | copy-start | bytes 98308
  0.6 8.3 %copy-start.8 = (s32[1,1,8192]{2,1,0:T(1,128)S(1)}, s32[1,1,8192]{2,1,0:T(1,128)}, u32[]{:S(2)}) copy-start(s32[1,1,8192]{2,1,0:T(1,128)} %param.13) | copy-start | bytes 98308
  2.4 10.1 %collective-permute-start = (f32[18432]{0:T(1024)S(1)}, f32[18432]{0:T(1024)S(1)}, u32[]{:S(2)}, u32[]{:S(2)}) collective-permute-start(f32[18432]{0:T(1024)S(1)} %get-tuple-element.38), channel_id=1, source_target_pairs={{4,8},{12,16},{20,24},{8,4},{16,12},{24,20},{5,9},{13,17},{21,25},... | collective-permute-start | bytes 221192 | tf_op jit(solution)/shard_map/ppermute | solution.py:515
  3.1 9.4 %collective-permute-start.1 = (f32[18432]{0:T(1024)S(1)}, f32[18432]{0:T(1024)S(1)}, u32[]{:S(2)}, u32[]{:S(2)}) collective-permute-start(f32[18432]{0:T(1024)S(1)} %get-tuple-element.39), channel_id=1, source_target_pairs={{0,4},{8,12},{16,20},{24,28},{4,0},{12,8},{20,16},{28,24},{1,5},{9... | collective-permute-start | bytes 221192 | tf_op jit(solution)/shard_map/ppermute | solution.py:515
  10.7 1.9 %copy-start = (f32[3,128,512]{2,1,0:T(8,128)S(1)}, f32[3,128,512]{2,1,0:T(8,128)}, u32[]{:S(2)}) copy-start(f32[3,128,512]{2,1,0:T(8,128)} %param.14) | copy-start | bytes 2359300
  10.7 1.9 %copy-start.3 = (f32[128,512]{1,0:T(8,128)S(1)}, f32[128,512]{1,0:T(8,128)}, u32[]{:S(2)}) copy-start(f32[128,512]{1,0:T(8,128)} %param.15) | copy-start | bytes 786436
  12.5 0.8 copy-start.4
  12.5 0.9 copy-start.5
  12.5 0.9 copy-start.7
  12.7 4.5 %copy-start.9 = (s32[4,16,9]{1,0,2:T(4,128)S(1)}, s32[4,16,9]{1,0,2:T(4,128)}, u32[]{:S(2)}) copy-start(s32[4,16,9]{1,0,2:T(4,128)} %param.11) | copy-start | bytes 6916
  13.6 5.1 %collective-permute-start.2 = (f32[6016]{0:T(1024)S(1)}, f32[6016]{0:T(1024)S(1)}, u32[]{:S(2)}, u32[]{:S(2)}) collective-permute-start(f32[6016]{0:T(1024)S(1)} %get-tuple-element.44), channel_id=1, source_target_pairs={{1,2},{2,1},{5,6},{6,5},{9,10},{10,9},{13,14},{14,13},{17,18},{18,... | collective-permute-start | bytes 72200 | tf_op jit(solution)/shard_map/ppermute | solution.py:515
  14.2 4.5 %collective-permute-start.3 = (f32[6016]{0:T(1024)S(1)}, f32[6016]{0:T(1024)S(1)}, u32[]{:S(2)}, u32[]{:S(2)}) collective-permute-start(f32[6016]{0:T(1024)S(1)} %get-tuple-element.45), channel_id=1, source_target_pairs={{0,1},{2,3},{1,0},{3,2},{4,5},{6,7},{5,4},{7,6},{8,9},{10,11},{9,8... | collective-permute-start | bytes 72200 | tf_op jit(solution)/shard_map/ppermute | solution.py:515
  40.9 18.0 %all-to-all-start = ((f32[32,24,128]{2,1,0:T(8,128)}), f32[32,24,128]{2,1,0:T(8,128)S(1)}, u32[]{:S(2)}, u32[]{:S(2)}) async-start(f32[32,24,128]{2,1,0:T(8,128)} %pack.1), calls=%async_computation | async-start | bytes 786432 | tf_op jit(solution)/shard_map/all_to_all | solution.py:579
  58.9 1.3 %copy-start.1 = (f32[32,24,128]{2,1,0:T(8,128)}, f32[32,24,128]{2,1,0:T(8,128)S(1)}, u32[]{:S(2)}) copy-start(f32[32,24,128]{2,1,0:T(8,128)S(1)} %all-to-all-done) | copy-start | bytes 1179652
  70.6 4.1 %collective-permute-start.4 = (f32[3,4,512]{2,1,0:T(4,128)}, f32[3,4,512]{2,1,0:T(4,128)S(1)}, u32[]{:S(2)}, u32[]{:S(2)}) collective-permute-start(f32[3,4,512]{2,1,0:T(4,128)} %get-tuple-element.13), channel_id=1, source_target_pairs={{4,8},{12,16},{20,24},{8,4},{16,12},{24,20},{5,9},{13,17},{21,25},... | collective-permute-start | bytes 73736 | tf_op jit(solution)/shard_map/ppermute | solution.py:515
  71.3 4.2 %collective-permute-start.5 = (f32[3,4,512]{2,1,0:T(4,128)}, f32[3,4,512]{2,1,0:T(4,128)S(1)}, u32[]{:S(2)}, u32[]{:S(2)}) collective-permute-start(f32[3,4,512]{2,1,0:T(4,128)} %get-tuple-element.14), channel_id=1, source_target_pairs={{0,4},{8,12},{16,20},{24,28},{4,0},{12,8},{20,16},{28,24},{1,5},{9... | collective-permute-start | bytes 73736 | tf_op jit(solution)/shard_map/ppermute | solution.py:515
  76.7 2.9 %collective-permute-start.7 = (f32[3,136,4]{2,1,0:T(8,128)S(1)}, f32[3,136,4]{2,1,0:T(8,128)S(1)}, u32[]{:S(2)}, u32[]{:S(2)}) collective-permute-start(f32[3,136,4]{2,1,0:T(8,128)S(1)} %broadcast_select_fusion.2), channel_id=1, source_target_pairs={{0,1},{2,3},{1,0},{3,2},{4,5},{6,7},{5,4},{7,6},{8,9},{10,11},{9,8... | collective-permute-start | bytes 19592 | tf_op jit(solution)/shard_map/ppermute | solution.py:515
  76.9 2.7 %copy-start.2 = (f32[3,128,512]{2,1,0:T(8,128)S(1)}, f32[3,128,512]{2,1,0:T(8,128)}, u32[]{:S(2)}) copy-start(f32[3,128,512]{2,1,0:T(8,128)} %get-tuple-element.15) | copy-start | bytes 2359300
  76.9 2.7 %collective-permute-start.6 = (f32[3,136,4]{2,1,0:T(8,128)S(1)}, f32[3,136,4]{2,1,0:T(8,128)S(1)}, u32[]{:S(2)}, u32[]{:S(2)}) collective-permute-start(f32[3,136,4]{2,1,0:T(8,128)S(1)} %get-tuple-element.25), channel_id=1, source_target_pairs={{1,2},{2,1},{5,6},{6,5},{9,10},{10,9},{13,14},{14,13},{17,18},{18,... | collective-permute-start | bytes 19592 | tf_op jit(solution)/shard_map/ppermute | solution.py:515
